TPU v7x, 128 devices: a whole 4x4x4 slice. The times are simulated.
128 devices in a mesh: dev: 32 (over y, x, core), ka: 4 (over z).
Axes of the slice: x: 4, y: 4, z: 4, core: 2. Of those that a mesh axis runs over, the one named last changes fastest.
Arguments:
- tile_data: float32 [8192, 128, 128], P(('dev', 'ka')), may hold values from -0.25 to 0.25
- tile_row: int32 [128, 64], P(('dev', 'ka')), may hold values from 0 to 31
- tile_col: int32 [128, 64], P(('dev', 'ka')), may hold values from 0 to 63
- tile_count: int32 [128], P(('dev', 'ka')), may hold values from 10 to 64, as said below
- touched: int32 [128, 64], P(('dev', 'ka')), may hold values from 0 to 511, as said below
- owner_map: int32 [512], replicated, may hold values from 0 to 511, as said below
- observed: float32 [4096, 128, 64], P(('dev', 'ka')), may hold values from -6 to 6
- start_x: float32 [8192, 128, 64], P(('dev', 'ka')), may hold values from -6 to 6
- start_u: float32 [8192, 128, 64], P(('dev', 'ka')), may hold values from -4 to 4
Outputs:
- final_x: float32 [8192, 128, 64], P(('dev', 'ka'))
- final_u: float32 [8192, 128, 64], P(('dev', 'ka'))
- z_keeper_agreed: float32 [512, 128, 64], P(('dev', 'ka'))
- primal_gap: float32 [64], replicated
Inputs may be any that keep to these rules, and one draw needn't show every extreme that they name: Shard s uses its first tile_count[s] slots; each count is at least 10 and at most 64, and some shard has exactly 64. `touched`: A shard's 64 entries are distinct column blocks. The owner of block j is shard owner_map[j] // 4; a shard touches at most one block of any one owner, and every shard touches exactly one block of some owner. `owner_map`: A permutation of 0 to 511.
All inputs are finite; a program needn't handle non-finite values.
Results may differ from a plain program's by a relative error of at most 0.0003.
Values sent between devices are 32-bit elements.
A program may use at most 128 MiB of HBM per device.

v0:
```python
import functools
import math

import jax
import jax.numpy as jnp
from jax import lax
from jax.sharding import Mesh
from jax.sharding import PartitionSpec as P

ITERS = 2
CG_STEPS = 4
DEV_KA = ("dev_0", "dev_1", "dev_2", "ka")


EXACTNESS = lax.Precision.HIGHEST
PENALTY = 1.0
COUPLING = 1.0


def by_axis(array, axes):
    return functools.reduce(lax.psum, axes, array)


def shrink(amount, cutoff):
    return amount - jnp.clip(amount, -cutoff, cutoff)


def tile_pass(tile_data, row_ids, col_ids, in_count, source, out_rows, forward):
    group_size = math.gcd(32, tile_data.shape[0])
    rounds = (in_count + group_size - 1) // group_size
    initial = jnp.zeros((out_rows,) + source.shape[1:], jnp.float32)

    def add_group(number, summed):
        offset = number * group_size
        tiles_now = lax.dynamic_slice_in_dim(tile_data, offset, group_size, 0)
        rows_now = lax.dynamic_slice_in_dim(row_ids, offset, group_size, 0)
        cols_now = lax.dynamic_slice_in_dim(col_ids, offset, group_size, 0)
        in_use = (offset + jnp.arange(group_size, dtype=jnp.int32) < in_count).astype(jnp.float32)
        if forward:
            product = jnp.einsum("tij,tjr->tir", tiles_now, source[cols_now], precision=EXACTNESS)
            landing = rows_now
        else:
            product = jnp.einsum("tji,tjr->tir", tiles_now, source[rows_now], precision=EXACTNESS)
            landing = cols_now
        return summed.at[landing].add(product * in_use[:, None, None])

    return lax.fori_loop(0, rounds, add_group, initial)


def conjugate(tile_data, row_ids, col_ids, in_count, row_blocks, rhs_side, begin):

    def operate(vector):
        image_rows = tile_pass(tile_data, row_ids, col_ids, in_count, vector, row_blocks, True)
        back_cols = tile_pass(
            tile_data, row_ids, col_ids, in_count, image_rows, vector.shape[0], False
        )
        return back_cols + COUPLING * vector

    iterate = begin
    residual = rhs_side - operate(begin)
    direction = residual
    norm_now = jnp.sum(residual * residual, axis=(0, 1))
    for cg_step in range(CG_STEPS):
        mapped = operate(direction)
        step_size = norm_now / jnp.sum(direction * mapped, axis=(0, 1))
        iterate = iterate + step_size * direction
        residual = residual - step_size * mapped
        norm_next = jnp.sum(residual * residual, axis=(0, 1))
        direction = residual + norm_next / norm_now * direction
        norm_now = norm_next
    return iterate


def on_device(
    tile_data, tile_row, tile_col, tile_count, touched, owner_map, observed, start_x, start_u
):
    shards = lax.axis_size(DEV_KA)
    local_cols = touched.shape[1]
    col_blocks = owner_map.shape[0]
    col_dev = col_blocks // shards
    capacity = max(1, (local_cols + shards - 1) // shards)
    row_ids = tile_row[0]
    col_ids = tile_col[0]
    in_count = tile_count[0]
    wanted = touched[0]
    row_blocks = observed.shape[0]
    block_shape = start_x.shape[1:]
    matches = (wanted[:, None] == jnp.arange(col_blocks, dtype=jnp.int32)[None, :]).astype(
        jnp.int32
    )
    position = jnp.sum(matches * owner_map[None, :], axis=1)
    owner = position // col_dev
    local_slot = position - owner * col_dev
    slot_order = jnp.arange(local_cols, dtype=jnp.int32)
    earlier = (owner[:, None] == owner[None, :]) & (slot_order[:, None] > slot_order[None, :])
    mailbox = owner * capacity + jnp.sum(earlier.astype(jnp.int32), axis=1)
    tags = jnp.full((shards * capacity,), -1, jnp.int32).at[mailbox].set(local_slot)
    arrived = lax.all_to_all(
        tags.reshape(shards, capacity), DEV_KA, split_axis=0, concat_axis=0, tiled=True
    ).reshape(-1)
    delivery_plan = (arrived[None, :] == jnp.arange(col_dev, dtype=jnp.int32)[:, None]).astype(
        jnp.float32
    )
    share = jnp.maximum(jnp.sum(delivery_plan, axis=1), 1.0)[:, None, None]
    pulled = tile_pass(tile_data, row_ids, col_ids, in_count, observed, local_cols, False)
    current_x = start_x
    current_u = start_u
    z_keeper_agreed = jnp.zeros((col_dev,) + block_shape, jnp.float32)
    difference = jnp.zeros_like(start_x)
    for outer_step in range(ITERS):
        merged = current_x + current_u
        outbox = jnp.zeros((shards * capacity,) + block_shape, jnp.float32).at[mailbox].set(merged)
        outbox = outbox.reshape((shards, capacity) + block_shape)
        inbox = lax.all_to_all(outbox, DEV_KA, split_axis=0, concat_axis=0, tiled=True)
        summed = jnp.einsum(
            "dy,ysh->dsh",
            delivery_plan,
            inbox.reshape((shards * capacity,) + block_shape),
            precision=EXACTNESS,
        )
        z_keeper_agreed = shrink(summed / share, PENALTY / (COUPLING * share))
        answers_back = jnp.einsum(
            "pu,pxa->uxa", delivery_plan, z_keeper_agreed, precision=EXACTNESS
        ).reshape((shards, capacity) + block_shape)
        returned = lax.all_to_all(answers_back, DEV_KA, split_axis=0, concat_axis=0, tiled=True)
        z_local = returned.reshape((shards * capacity,) + block_shape)[mailbox]
        difference = current_x - z_local
        current_u = current_u + difference
        rhs_side = pulled + COUPLING * (z_local - current_u)
        current_x = conjugate(
            tile_data, row_ids, col_ids, in_count, row_blocks, rhs_side, current_x
        )
    gap_total = by_axis(jnp.sum(difference * difference, axis=(0, 1)), DEV_KA)
    primal_gap = jnp.sqrt(gap_total / (shards * local_cols * block_shape[0]))
    return (current_x, current_u, z_keeper_agreed, primal_gap)


def solution(mesh):
    finer = Mesh(mesh.devices.reshape(4, 4, 2, mesh.shape["ka"]), ("dev_0", "dev_1", "dev_2", "ka"))
    placed = (
        P(DEV_KA, None, None),
        P(DEV_KA, None),
        P(DEV_KA, None),
        P(DEV_KA),
        P(DEV_KA, None),
        P(),
        P(DEV_KA, None, None),
        P(DEV_KA, None, None),
        P(DEV_KA, None, None),
    )
    return jax.shard_map(
        on_device,
        mesh=finer,
        in_specs=placed,
        out_specs=(P(DEV_KA, None, None), P(DEV_KA, None, None), P(DEV_KA, None, None), P()),
        check_vma=False,
    )
```

profile of v0, /device:TPU:1, one launch (start us, length us, event | category | flops | bytes accessed | tf_op | source)
XLA Modules:
  0.0 947.0 jit_solution(11465945133138843421)
XLA Ops:
  3.3 11.5 %all-to-all-start = ((s32[128,1,1]{2,1,0:T(1,128)}), s32[128,1,1]{2,1,0:T(1,128)S(1)}, u32[]{:S(2)}, u32[]{:S(2)}) async-start(s32[128,1,1]{2,1,0:T(1,128)} %copy.227), calls=%async_computation | async-start | bytes 131072 | tf_op jit(solution)/shard_map/all_to_all | solution.py:98
  28.5 10.2 %all-to-all-start.1 = ((f32[128,1,128,64]{2,3,1,0:T(8,128)}), f32[128,1,128,64]{2,3,1,0:T(8,128)}, u32[]{:S(2)}, u32[]{:S(2)}) async-start(f32[128,1,128,64]{2,3,1,0:T(8,128)} %bitcast.117), calls=%async_computation.1 | async-start | bytes 8388608 | tf_op jit(solution)/shard_map/all_to_all | solution.py:114
  39.5 11.0 %while.211 = (s32[]{:T(128)}, f32[32,128,64]{1,2,0:T(8,128)S(1)}, s32[]{:T(128)}, s32[64]{0:T(128)S(1)}, f32[64,128,128]{2,1,0:T(8,128)}, /*index=5*/s32[64]{0:T...) while((s32[]{:T(128)}, f32[32,128,64]{1,2,0:T(8,128)S(1)}, ...), condition=%wide.region_10.11_spmd, body=%wide.region_8.10_spmd.sunk | while | flops 403178784 | bytes 9442611 | solution.py:47
  55.1 42.9 %all-to-all-done.1 = f32[128,1,128,64]{2,3,1,0:T(8,128)} async-done(((f32[128,1,128,64]{2,3,1,0:T(8,128)}), f32[128,1,128,64]{2,3,1,0:T(8,128)}, u32[]{:S(2)}, u32[]{:S(2)}) %all-to-all-start.1) | async-done | bytes 4194336 | tf_op jit(solution)/shard_map/all_to_all | solution.py:114
  117.9 9.9 %while.210 = (s32[]{:T(128)}, f32[64,128,64]{1,2,0:T(8,128)}, s32[]{:T(128)}, s32[64]{0:T(128)S(1)}, f32[64,128,128]{2,1,0:T(8,128)}, /*index=5*/s32[64]{0:T(128...) while((s32[]{:T(128)}, f32[64,128,64]{1,2,0:T(8,128)}, ...), condition=%wide.region_2.3_spmd, body=%wide.region_0.2_spmd.sunk | while | flops 403178784 | bytes 9442611 | solution.py:47
  129.4 13.0 %while.212 = (s32[]{:T(128)}, f32[64,128,64]{1,2,0:T(8,128)}, s32[]{:T(128)}, s32[64]{0:T(128)S(1)}, f32[64,128,128]{2,1,0:T(8,128)}, /*index=5*/s32[64]{0:T(128...) while((s32[]{:T(128)}, f32[64,128,64]{1,2,0:T(8,128)}, ...), condition=%wide.region_13.14_spmd, body=%wide.region_11.13_spmd.sunk | while | flops 403178784 | bytes 9442611 | solution.py:47
  142.5 33.1 %all-to-all-done.2 = f32[128,1,128,64]{2,3,1,0:T(8,128)} async-done(((f32[128,1,128,64]{2,3,1,0:T(8,128)}), f32[128,1,128,64]{2,3,1,0:T(8,128)}, u32[]{:S(2)}, u32[]{:S(2)}) %all-to-all-start.2) | async-done | bytes 4194336 | tf_op jit(solution)/shard_map/all_to_all | solution.py:125
  190.9 14.3 %while.213 = (s32[]{:T(128)}, f32[32,128,64]{1,2,0:T(8,128)}, s32[]{:T(128)}, s32[64]{0:T(128)S(1)}, f32[64,128,128]{2,1,0:T(8,128)}, /*index=5*/s32[64]{0:T(128...) while((s32[]{:T(128)}, f32[32,128,64]{1,2,0:T(8,128)}, ...), condition=%wide.region_17.18_spmd, body=%wide.region_15.17_spmd.sunk | while | flops 403178784 | bytes 9442611 | solution.py:47
  209.9 13.0 %while.214 = (s32[]{:T(128)}, f32[64,128,64]{1,2,0:T(8,128)}, s32[]{:T(128)}, s32[64]{0:T(128)S(1)}, f32[64,128,128]{2,1,0:T(8,128)}, /*index=5*/s32[64]{0:T(128...) while((s32[]{:T(128)}, f32[64,128,64]{1,2,0:T(8,128)}, ...), condition=%wide.region_20.21_spmd, body=%wide.region_18.20_spmd.sunk | while | flops 403178784 | bytes 9442611 | solution.py:47
  231.7 14.1 %while.215 = (s32[]{:T(128)}, f32[32,128,64]{1,2,0:T(8,128)}, s32[]{:T(128)}, s32[64]{0:T(128)S(1)}, f32[64,128,128]{2,1,0:T(8,128)}, /*index=5*/s32[64]{0:T(128...) while((s32[]{:T(128)}, f32[32,128,64]{1,2,0:T(8,128)}, ...), condition=%wide.region_25.26_spmd, body=%wide.region_23.25_spmd.sunk | while | flops 403178784 | bytes 9442611 | solution.py:47
  250.6 13.0 %while.216 = (s32[]{:T(128)}, f32[64,128,64]{1,2,0:T(8,128)}, s32[]{:T(128)}, s32[64]{0:T(128)S(1)}, f32[64,128,128]{2,1,0:T(8,128)}, /*index=5*/s32[64]{0:T(128...) while((s32[]{:T(128)}, f32[64,128,64]{1,2,0:T(8,128)}, ...), condition=%wide.region_28.29_spmd, body=%wide.region_26.28_spmd.sunk | while | flops 403178784 | bytes 9442611 | solution.py:47
  274.0 14.1 %while.217 = (s32[]{:T(128)}, f32[32,128,64]{1,2,0:T(8,128)}, s32[]{:T(128)}, s32[64]{0:T(128)S(1)}, f32[64,128,128]{2,1,0:T(8,128)}, /*index=5*/s32[64]{0:T(128...) while((s32[]{:T(128)}, f32[32,128,64]{1,2,0:T(8,128)}, ...), condition=%wide.region_33.34_spmd, body=%wide.region_31.33_spmd.sunk | while | flops 403178784 | bytes 9442611 | solution.py:47
  292.9 13.0 %while.218 = (s32[]{:T(128)}, f32[64,128,64]{1,2,0:T(8,128)}, s32[]{:T(128)}, s32[64]{0:T(128)S(1)}, f32[64,128,128]{2,1,0:T(8,128)}, /*index=5*/s32[64]{0:T(128...) while((s32[]{:T(128)}, f32[64,128,64]{1,2,0:T(8,128)}, ...), condition=%wide.region_36.37_spmd, body=%wide.region_34.36_spmd.sunk | while | flops 403178784 | bytes 9442611 | solution.py:47
  315.3 14.3 %while.219 = (s32[]{:T(128)}, f32[32,128,64]{1,2,0:T(8,128)}, s32[]{:T(128)}, s32[64]{0:T(128)S(1)}, f32[64,128,128]{2,1,0:T(8,128)}, /*index=5*/s32[64]{0:T(128...) while((s32[]{:T(128)}, f32[32,128,64]{1,2,0:T(8,128)}, ...), condition=%wide.region_41.42_spmd, body=%wide.region_39.41_spmd.sunk | while | flops 403178784 | bytes 9442611 | solution.py:47
  334.4 13.0 %while.220 = (s32[]{:T(128)}, f32[64,128,64]{1,2,0:T(8,128)}, s32[]{:T(128)}, s32[64]{0:T(128)S(1)}, f32[64,128,128]{2,1,0:T(8,128)}, /*index=5*/s32[64]{0:T(128...) while((s32[]{:T(128)}, f32[64,128,64]{1,2,0:T(8,128)}, ...), condition=%wide.region_44.45_spmd, body=%wide.region_42.44_spmd.sunk | while | flops 403178784 | bytes 9442611 | solution.py:47
  360.7 10.0 %scatter_fusion.22 = f32[128,128,64]{1,2,0:T(8,128)} fusion(f32[128,128,64]{1,2,0:T(8,128)} %broadcast.519, s32[64]{0:T(128)S(1)} %copy-done.36, f32[64,128,64]{1,2,0:T(8,128)} %get-tuple-element.2057), kind=kCustom, calls=%fused_computation.46 | custom fusion | bytes 6291712 | tf_op jit(solution)/shard_map/scatter | solution.py:112
  370.8 113.7 %all-to-all-start.3 = ((f32[128,1,128,64]{2,3,1,0:T(8,128)}), f32[128,1,128,64]{2,3,1,0:T(8,128)}, u32[]{:S(2)}, u32[]{:S(2)}) async-start(f32[128,1,128,64]{2,3,1,0:T(8,128)} %bitcast.116), calls=%async_computation.3 | async-start | bytes 8388608 | tf_op jit(solution)/shard_map/all_to_all | solution.py:114
  487.2 56.5 %all-to-all-done.3 = f32[128,1,128,64]{2,3,1,0:T(8,128)} async-done(((f32[128,1,128,64]{2,3,1,0:T(8,128)}), f32[128,1,128,64]{2,3,1,0:T(8,128)}, u32[]{:S(2)}, u32[]{:S(2)}) %all-to-all-start.3) | async-done | bytes 4194336 | tf_op jit(solution)/shard_map/all_to_all | solution.py:114
  563.2 14.1 %while.221 = (s32[]{:T(128)}, f32[32,128,64]{1,2,0:T(8,128)}, s32[]{:T(128)}, s32[64]{0:T(128)S(1)}, f32[64,128,128]{2,1,0:T(8,128)}, /*index=5*/s32[64]{0:T(128...) while((s32[]{:T(128)}, f32[32,128,64]{1,2,0:T(8,128)}, ...), condition=%wide.region_49.50_spmd, body=%wide.region_47.49_spmd.sunk | while | flops 403178784 | bytes 9442611 | solution.py:47
  582.0 13.0 %while.222 = (s32[]{:T(128)}, f32[64,128,64]{1,2,0:T(8,128)}, s32[]{:T(128)}, s32[64]{0:T(128)S(1)}, f32[64,128,128]{2,1,0:T(8,128)}, /*index=5*/s32[64]{0:T(128...) while((s32[]{:T(128)}, f32[64,128,64]{1,2,0:T(8,128)}, ...), condition=%wide.region_52.53_spmd, body=%wide.region_50.52_spmd.sunk | while | flops 403178784 | bytes 9442611 | solution.py:47
  595.8 25.6 %all-to-all-done.4 = f32[128,1,128,64]{2,3,1,0:T(8,128)} async-done(((f32[128,1,128,64]{2,3,1,0:T(8,128)}), f32[128,1,128,64]{2,3,1,0:T(8,128)}, u32[]{:S(2)}, u32[]{:S(2)}) %all-to-all-start.4) | async-done | bytes 4194336 | tf_op jit(solution)/shard_map/all_to_all | solution.py:125
  625.8 9.3 add_subtract_fusion
  640.0 14.3 %while.223 = (s32[]{:T(128)}, f32[32,128,64]{1,2,0:T(8,128)}, s32[]{:T(128)}, s32[64]{0:T(128)S(1)}, f32[64,128,128]{2,1,0:T(8,128)}, /*index=5*/s32[64]{0:T(128...) while((s32[]{:T(128)}, f32[32,128,64]{1,2,0:T(8,128)}, ...), condition=%wide.region_56.57_spmd, body=%wide.region_54.56_spmd.sunk | while | flops 403178784 | bytes 9442611 | solution.py:47
  659.1 13.1 %while.224 = (s32[]{:T(128)}, f32[64,128,64]{1,2,0:T(8,128)}, s32[]{:T(128)}, s32[64]{0:T(128)S(1)}, f32[64,128,128]{2,1,0:T(8,128)}, /*index=5*/s32[64]{0:T(128...) while((s32[]{:T(128)}, f32[64,128,64]{1,2,0:T(8,128)}, ...), condition=%wide.region_59.60_spmd, body=%wide.region_57.59_spmd.sunk | while | flops 403178784 | bytes 9442611 | solution.py:47
  680.9 14.1 %while.225 = (s32[]{:T(128)}, f32[32,128,64]{1,2,0:T(8,128)}, s32[]{:T(128)}, s32[64]{0:T(128)S(1)}, f32[64,128,128]{2,1,0:T(8,128)}, /*index=5*/s32[64]{0:T(128...) while((s32[]{:T(128)}, f32[32,128,64]{1,2,0:T(8,128)}, ...), condition=%wide.region_64.65_spmd, body=%wide.region_62.64_spmd.sunk | while | flops 403178784 | bytes 9442611 | solution.py:47
  699.8 13.1 %while.226 = (s32[]{:T(128)}, f32[64,128,64]{1,2,0:T(8,128)}, s32[]{:T(128)}, s32[64]{0:T(128)S(1)}, f32[64,128,128]{2,1,0:T(8,128)}, /*index=5*/s32[64]{0:T(128...) while((s32[]{:T(128)}, f32[64,128,64]{1,2,0:T(8,128)}, ...), condition=%wide.region_67.68_spmd, body=%wide.region_65.67_spmd.sunk | while | flops 403178784 | bytes 9442611 | solution.py:47
  723.4 14.2 %while.227 = (s32[]{:T(128)}, f32[32,128,64]{1,2,0:T(8,128)}, s32[]{:T(128)}, s32[64]{0:T(128)S(1)}, f32[64,128,128]{2,1,0:T(8,128)}, /*index=5*/s32[64]{0:T(128...) while((s32[]{:T(128)}, f32[32,128,64]{1,2,0:T(8,128)}, ...), condition=%wide.region_72.73_spmd, body=%wide.region_70.72_spmd.sunk | while | flops 403178784 | bytes 9442611 | solution.py:47
  742.3 13.0 %while.228 = (s32[]{:T(128)}, f32[64,128,64]{1,2,0:T(8,128)}, s32[]{:T(128)}, s32[64]{0:T(128)S(1)}, f32[64,128,128]{2,1,0:T(8,128)}, /*index=5*/s32[64]{0:T(128...) while((s32[]{:T(128)}, f32[64,128,64]{1,2,0:T(8,128)}, ...), condition=%wide.region_75.76_spmd, body=%wide.region_73.75_spmd.sunk | while | flops 403178784 | bytes 9442611 | solution.py:47
  764.6 14.2 %while.229 = (s32[]{:T(128)}, f32[32,128,64]{1,2,0:T(8,128)}, s32[]{:T(128)}, s32[64]{0:T(128)S(1)}, f32[64,128,128]{2,1,0:T(8,128)}, /*index=5*/s32[64]{0:T(128...) while((s32[]{:T(128)}, f32[32,128,64]{1,2,0:T(8,128)}, ...), condition=%wide.region_80.81_spmd, body=%wide.region_78.80_spmd.sunk | while | flops 403178784 | bytes 9442611 | solution.py:47
  783.6 13.0 %while.230 = (s32[]{:T(128)}, f32[64,128,64]{1,2,0:T(8,128)}, s32[]{:T(128)}, s32[64]{0:T(128)S(1)}, f32[64,128,128]{2,1,0:T(8,128)}, /*index=5*/s32[64]{0:T(128...) while((s32[]{:T(128)}, f32[64,128,64]{1,2,0:T(8,128)}, ...), condition=%wide.region_83.84_spmd, body=%wide.region_81.83_spmd.sunk | while | flops 403178784 | bytes 9442611 | solution.py:47
  813.3 117.5 %psum.29 = f32[64]{0:T(128)S(1)} all-reduce(f32[64]{0:T(128)S(1)} %psum.28), channel_id=1, replica_groups=mesh['dev_0'=4,'dev_1'=4,'dev_2'=2,'ka'=4] {'dev_1'}, use_global_device_ids=true, to_apply=%region_87.88 | all-reduce | flops 64 | bytes 512 | tf_op jit(solution)/shard_map/psum | solution.py:21
  934.5 11.6 %psum.31 = f32[64]{0:T(128)S(1)} all-reduce(f32[64]{0:T(128)S(1)} %psum.30), channel_id=1, replica_groups=mesh['dev_0'=4,'dev_1'=4,'dev_2'=2,'ka'=4] {'ka'}, use_global_device_ids=true, to_apply=%region_89.90 | all-reduce | flops 64 | bytes 512 | tf_op jit(solution)/shard_map/psum | solution.py:21
  (320 shorter events, 499.5 us)
Async XLA Ops:
  1.7 50.8 %copy-start.35 = (s32[64]{0:T(128)}, s32[64]{0:T(128)S(1)}, u32[]{:S(2)}) copy-start(s32[64]{0:T(128)S(1)} %fusion.149) | copy-start | bytes 772
  3.3 25.3 %all-to-all-start = ((s32[128,1,1]{2,1,0:T(1,128)}), s32[128,1,1]{2,1,0:T(1,128)S(1)}, u32[]{:S(2)}, u32[]{:S(2)}) async-start(s32[128,1,1]{2,1,0:T(1,128)} %copy.227), calls=%async_computation | async-start | bytes 131072 | tf_op jit(solution)/shard_map/all_to_all | solution.py:98
  28.5 11.0 %copy-start.30 = (s32[1,64]{1,0:T(1,128)S(1)}, s32[1,64]{1,0:T(1,128)}, u32[]{:S(2)}) copy-start(s32[1,64]{1,0:T(1,128)} %param.53) | copy-start | bytes 772
  28.5 11.0 %copy-start.31 = (s32[1,64]{1,0:T(1,128)S(1)}, s32[1,64]{1,0:T(1,128)}, u32[]{:S(2)}) copy-start(s32[1,64]{1,0:T(1,128)} %param.52) | copy-start | bytes 772
  28.5 69.4 %all-to-all-start.1 = ((f32[128,1,128,64]{2,3,1,0:T(8,128)}), f32[128,1,128,64]{2,3,1,0:T(8,128)}, u32[]{:S(2)}, u32[]{:S(2)}) async-start(f32[128,1,128,64]{2,3,1,0:T(8,128)} %bitcast.117), calls=%async_computation.1 | async-start | bytes 8388608 | tf_op jit(solution)/shard_map/all_to_all | solution.py:114
  52.6 123.1 %copy-start.34 = (s32[1024]{0:T(1024)}, s32[1024]{0:T(1024)S(1)}, u32[]{:S(2)}) copy-start(s32[1024]{0:T(1024)S(1)} %pad_clamp_fusion.21) | copy-start | bytes 12292
  54.9 48.8 %copy-start.32 = (s32[128]{0:T(128)}, s32[128]{0:T(128)S(1)}, u32[]{:S(2)}) copy-start(s32[128]{0:T(128)S(1)} %reduce) | copy-start | bytes 1540
  55.0 48.7 %copy-start.41 = (f32[4]{0:T(128)}, f32[4]{0:T(128)S(1)}, u32[]{:S(2)}) copy-start(f32[4]{0:T(128)S(1)} %get-tuple-element.2113) | copy-start | bytes 52
  55.1 48.7 %copy-start.37 = (f32[4]{0:T(128)}, f32[4]{0:T(128)S(1)}, u32[]{:S(2)}) copy-start(f32[4]{0:T(128)S(1)} %get-tuple-element.2066) | copy-start | bytes 52
  55.1 48.7 %copy-start.39 = (f32[4]{0:T(128)}, f32[4]{0:T(128)S(1)}, u32[]{:S(2)}) copy-start(f32[4]{0:T(128)S(1)} %get-tuple-element.2067) | copy-start | bytes 52
  110.0 65.6 %all-to-all-start.2 = ((f32[128,1,128,64]{2,3,1,0:T(8,128)}), f32[128,1,128,64]{2,3,1,0:T(8,128)}, u32[]{:S(2)}, u32[]{:S(2)}) async-start(f32[128,1,128,64]{2,3,1,0:T(8,128)} %copy.230), calls=%async_computation.2 | async-start | bytes 8388608 | tf_op jit(solution)/shard_map/all_to_all | solution.py:125
  175.6 4.4 copy-start
  223.0 3.0 copy-start.3
  263.6 3.0 copy-start.4
  263.6 3.5 copy-start.25
  305.9 3.0 copy-start.20
  347.4 3.5 copy-start.11
  358.1 126.3 %copy-start.29 = (f32[64,128,64]{1,2,0:T(8,128)}, f32[64,128,64]{1,2,0:T(8,128)S(1)}, u32[]{:S(2)}) copy-start(f32[64,128,64]{1,2,0:T(8,128)S(1)} %get-tuple-element.2058) | copy-start | bytes 6291460
  370.8 172.9 %all-to-all-start.3 = ((f32[128,1,128,64]{2,3,1,0:T(8,128)}), f32[128,1,128,64]{2,3,1,0:T(8,128)}, u32[]{:S(2)}, u32[]{:S(2)}) async-start(f32[128,1,128,64]{2,3,1,0:T(8,128)} %bitcast.116), calls=%async_computation.3 | async-start | bytes 8388608 | tf_op jit(solution)/shard_map/all_to_all | solution.py:114
  484.4 59.3 %copy-start.33 = (s32[128]{0:T(128)S(1)}, s32[128]{0:T(128)}, u32[]{:S(2)}) copy-start(s32[128]{0:T(128)} %copy-done.32) | copy-start | bytes 1540
  484.5 59.2 %copy-start.38 = (f32[4]{0:T(128)S(1)}, f32[4]{0:T(128)}, u32[]{:S(2)}) copy-start(f32[4]{0:T(128)} %copy-done.37) | copy-start | bytes 52
  484.5 59.2 %copy-start.40 = (f32[4]{0:T(128)S(1)}, f32[4]{0:T(128)}, u32[]{:S(2)}) copy-start(f32[4]{0:T(128)} %copy-done.39) | copy-start | bytes 52
  484.5 59.2 %copy-start.42 = (f32[4]{0:T(128)S(1)}, f32[4]{0:T(128)}, u32[]{:S(2)}) copy-start(f32[4]{0:T(128)} %copy-done.41) | copy-start | bytes 52
  555.8 65.6 %all-to-all-start.4 = ((f32[128,1,128,64]{2,3,1,0:T(8,128)}), f32[128,1,128,64]{2,3,1,0:T(8,128)}, u32[]{:S(2)}, u32[]{:S(2)}) async-start(f32[128,1,128,64]{2,3,1,0:T(8,128)} %copy.242), calls=%async_computation.4 | async-start | bytes 8388608 | tf_op jit(solution)/shard_map/all_to_all | solution.py:125
  621.3 4.5 copy-start.1
  672.1 3.0 copy-start.6
  712.9 3.0 copy-start.7
  712.9 3.5 copy-start.27
  755.3 3.0 copy-start.22
  796.6 2.9 copy-start.8
  796.6 3.5 copy-start.16
  800.1 5.5 copy-start.43
  (17 other events, 36.9 us)
where the time goes:
time: 964 us; the launch traced here: 947 us
  local copies, waits for them, and re-layouts  188 us (20%)
  other arithmetic  181 us (19%)
  waiting for transfers between devices  158 us (16%)
  starting transfers between devices  148 us (15%)
  blocking collectives  140 us (15%)
  matrix products  126 us (13%)
    psum x4, blocking collectives, by_axis(): return functools.reduce(lax.psum, axes, array)  140 us
    all_to_all x2, starting transfers between devices, on_device(): lax.all_to_all(outbox, DEV_KA, split_axis=0, concat_axis=0, tiled=True)  124 us
    all_to_all x2, waiting for transfers between devices, on_device(): lax.all_to_all(outbox, DEV_KA, split_axis=0, concat_axis=0, tiled=True)  99.4 us
    scatter-add x21, other arithmetic, add_group(): return summed.at[landing].add(product * in_use[:, None, None])  98.2 us
    all_to_all x2, waiting for transfers between devices, on_device(): lax.all_to_all(answers_back, DEV_KA, split_axis=0, concat_axis=0, tiled=T...  58.7 us
    while x19, local copies, waits for them, and re-layouts, tile_pass(): return lax.fori_loop(0, rounds, add_group, initial)  57 us
    dot_general x10, matrix products, add_group(): jnp.einsum('tij,tjr->tir', tiles_now, source[cols_now], precision=EXACTNESS)  55.5 us
    dot_general x11, matrix products, add_group(): jnp.einsum('tji,tjr->tir', tiles_now, source[rows_now], precision=EXACTNESS)  55.4 us
  transfers between devices with their start and end apart: 5, of which 4 were waited for; matrix products, arithmetic and copies ran while one was open for 10% of the time, Pallas kernels for 0%

commit v1 on v0

v1 whole, which is shorter than its diff:
```python
import functools

import jax
import jax.numpy as jnp
from jax import lax
from jax.experimental import pallas as pl
from jax.experimental.pallas import tpu as pltpu
from jax.sharding import PartitionSpec as P

ITERS = 2
CG_STEPS = 4
GROUP = 8
AXES = ("dev", "ka")
F32 = jnp.float32
BF16 = jnp.bfloat16


def split_store(ref, index, value):
    rows = value.shape[0]
    high = value.astype(BF16)
    low = (value - high.astype(F32)).astype(BF16)
    ref[index, :rows, :] = high
    ref[index, rows:, :] = low


def join(wide, rows, cols):
    return (wide[:rows, :cols] + wide[:rows, cols:]) + wide[rows:, :cols]


def tile_plan(rows, cols, count):
    tiles = rows.shape[0]
    place = jnp.arange(tiles, dtype=jnp.int32)
    used = place < count

    def order(key):
        code = jnp.where(used, key, tiles) * tiles + place
        rank = jnp.sum((code[None, :] < code[:, None]).astype(jnp.int32), axis=1)
        pick = rank[None, :] == place[:, None]
        return rank, pick

    def take(pick, values):
        return jnp.sum(jnp.where(pick, values[None, :], 0), axis=1)

    row_key = jnp.where(used, rows, tiles)
    col_key = jnp.where(used, cols, tiles)
    rank_f, pick_f = order(rows)
    rank_b, pick_b = order(cols)
    row_sorted = take(pick_f, row_key)
    col_sorted = take(pick_b, col_key)
    before = lambda s: jnp.concatenate([jnp.full((1,), -1, jnp.int32), s[:-1]])
    after = lambda s: jnp.concatenate([s[1:], jnp.full((1,), -1, jnp.int32)])
    keep_f = (row_sorted == before(row_sorted)).astype(jnp.int32)
    keep_b = (col_sorted == before(col_sorted)).astype(jnp.int32)
    ends_f = ((row_sorted != after(row_sorted)) & (row_sorted < tiles)).astype(jnp.int32)
    last_of_row = jnp.max(jnp.where(row_key[:, None] == row_key[None, :], rank_f[None, :], 0), axis=1)
    column = jnp.arange(tiles, dtype=jnp.int32)
    last_of_col = jnp.max(jnp.where(col_key[None, :] == column[:, None], rank_b[None, :] + 1, 0), axis=1)
    last_of_col = jnp.where(last_of_col == 0, tiles, last_of_col - 1)
    return jnp.stack([
        take(pick_f, place), take(pick_f, cols), keep_f, ends_f, jnp.minimum(row_sorted, 31),
        take(pick_b, place), take(pick_b, last_of_row), keep_b, last_of_col,
    ])


def make_passes(plan, tiles_hl, image_hl, back, slots, targets, blk):
    count = slots

    def forward(source_hl, observed=None, square=False):
        def group(g, carry):
            acc, total = carry
            for n in range(GROUP):
                k = g * GROUP + n
                tile = plan[0, k]
                wide = lax.dot_general(
                    source_hl[plan[1, k]], tiles_hl[tile], (((1,), (1,)), ((), ())),
                    preferred_element_type=F32)
                acc = jnp.where(plan[2, k] > 0, acc, 0.0) + join(wide, targets, blk)
                if square:
                    total = total + jnp.where(plan[3, k] > 0, acc * acc, 0.0)
                elif observed is not None:
                    split_store(image_hl, k, observed[plan[4, k]] - acc)
                else:
                    split_store(image_hl, k, acc)
            return acc, total

        zero = jnp.zeros((targets, blk), F32)
        return lax.fori_loop(0, count // GROUP, group, (zero, zero))[1]

    def backward():
        def group(g, acc):
            for n in range(GROUP):
                k = g * GROUP + n
                both = tiles_hl[plan[5, k]]
                weights = jnp.concatenate([both[:blk], both[blk:]], axis=1)
                wide = jnp.dot(image_hl[plan[6, k]], weights, preferred_element_type=F32)
                acc = jnp.where(plan[7, k] > 0, acc, 0.0) + join(wide, targets, blk)
                back[k] = acc
            return acc

        lax.fori_loop(0, count // GROUP, group, jnp.zeros((targets, blk), F32))

    return forward, backward


def over_slots(slots, body, *init):
    step = 4

    def group(g, carry):
        for n in range(step):
            carry = body(g * step + n, *carry)
        return carry

    return lax.fori_loop(0, slots // step, group, init)


def total_of(value):
    return jnp.sum(value, axis=1, keepdims=True)


def solve_kernel(first, *refs):
    if first:
        (plan, tiles, observed, x, u, z, x_out, r_out, u_out, gap_out,
         tiles_hl, p, p_hl, image_hl, back) = refs
    else:
        (plan, tiles, x, u, z, z_before, r_in, x_out, u_out, gap_out,
         r_out, tiles_hl, p, p_hl, image_hl, back) = refs
    slots, targets, blk = x.shape
    zero = jnp.zeros((targets, blk), F32)
    back[slots] = zero

    def split_tile(t, _):
        split_store(tiles_hl, t, tiles[t])
        return _

    lax.fori_loop(0, slots, split_tile, 0)
    forward, backward = make_passes(plan, tiles_hl, image_hl, back, slots, targets, blk)

    if first:
        def load_x(c, _):
            split_store(p_hl, c, x[c])
            return (_,)

        over_slots(slots, load_x, 0)
        forward(p_hl, observed=observed)
        backward()

    def begin(c, rr, gap):
        diff = x[c] - z[c]
        u_new = u[c] + diff
        u_out[c] = u_new
        if first:
            r = back[plan[8, c]] + (z[c] - u_new) - x[c]
        else:
            r = r_in[c] + ((z[c] - u_new) - (z_before[c] - u[c]))
        r_out[c] = r
        p[c] = r
        split_store(p_hl, c, r)
        x_out[c] = x[c]
        return rr + r * r, gap + diff * diff

    rr, gap = over_slots(slots, begin, zero, zero)
    gap_out[...] = gap
    rr = total_of(rr)

    def advance(a, update_p, rr):
        def move(c, nn):
            r = r_out[c] - a * (back[plan[8, c]] + p[c])
            r_out[c] = r
            x_out[c] = x_out[c] + a * p[c]
            return (nn + r * r,)

        (nn,) = over_slots(slots, move, zero)
        nn = total_of(nn)
        if update_p:
            ratio = nn / rr

            def turn(c, _):
                value = r_out[c] + ratio * p[c]
                p[c] = value
                split_store(p_hl, c, value)
                return (_,)

            over_slots(slots, turn, 0)
        return nn

    def length(c, pq):
        value = p[c]
        return (pq + value * (back[plan[8, c]] + value),)

    def step(_, rr):
        forward(p_hl)
        backward()
        (pq,) = over_slots(slots, length, zero)
        return advance(rr / total_of(pq), True, rr)

    rr = lax.fori_loop(0, CG_STEPS - 1, step, rr)
    if first:
        forward(p_hl)
        backward()
        (pq,) = over_slots(slots, length, zero)
        advance(rr / total_of(pq), False, rr)
    else:
        square = forward(p_hl, square=True)

        def own(c, total):
            return (total + p[c] * p[c],)

        (pp,) = over_slots(slots, own, square)
        a = rr / total_of(pp)

        def finish(c, _):
            x_out[c] = x_out[c] + a * p[c]
            return (_,)

        over_slots(slots, finish, 0)


def solve(first, plan, *arrays):
    tiles = arrays[0]
    x = arrays[2] if first else arrays[1]
    slots, targets, blk = x.shape
    like = jax.ShapeDtypeStruct(x.shape, F32)
    gap = jax.ShapeDtypeStruct((targets, blk), F32)
    work = [
        pltpu.VMEM((tiles.shape[0], 2 * blk, blk), BF16),
        pltpu.VMEM(x.shape, F32),
        pltpu.VMEM((slots, 2 * targets, blk), BF16),
        pltpu.VMEM((slots, 2 * targets, blk), BF16),
        pltpu.VMEM((slots + 1, targets, blk), F32),
    ]
    if first:
        outs = (like, like, like, gap)
    else:
        outs = (like, like, gap)
        work = [pltpu.VMEM(x.shape, F32)] + work
    whole = pl.BlockSpec(memory_space=pltpu.VMEM)
    return pl.pallas_call(
        functools.partial(solve_kernel, first),
        out_shape=outs,
        in_specs=[pl.BlockSpec(memory_space=pltpu.SMEM)] + [whole] * len(arrays),
        out_specs=tuple(whole for _ in outs),
        scratch_shapes=work,
        compiler_params=pltpu.CompilerParams(vmem_limit_bytes=60 * 1024 * 1024),
        name="solve_first" if first else "solve_next",
    )(plan, *arrays)


def shrink(amount, cutoff):
    return amount - jnp.clip(amount, -cutoff, cutoff)


def on_device(tile_data, tile_row, tile_col, tile_count, touched, owner_map, observed, start_x, start_u):
    shards = lax.axis_size(AXES)
    local_cols = touched.shape[1]
    col_blocks = owner_map.shape[0]
    col_dev = col_blocks // shards
    plan = tile_plan(tile_row[0], tile_col[0], tile_count[0])
    wanted = touched[0]
    matches = (wanted[:, None] == jnp.arange(col_blocks, dtype=jnp.int32)[None, :]).astype(jnp.int32)
    position = jnp.sum(matches * owner_map[None, :], axis=1)
    owner = position // col_dev
    local_slot = position - owner * col_dev
    tags = jnp.full((shards,), -1, jnp.int32).at[owner].set(local_slot)
    arrived = lax.all_to_all(tags.reshape(shards, 1), AXES, split_axis=0, concat_axis=0, tiled=True).reshape(-1)
    delivery = (arrived[None, :] == jnp.arange(col_dev, dtype=jnp.int32)[:, None]).astype(F32)
    share = jnp.maximum(jnp.sum(delivery, axis=1), 1.0)[:, None, None]
    flip = lambda a: jnp.swapaxes(a, 1, 2)
    x, u, b = flip(start_x), flip(start_u), flip(observed)
    block = x.shape[1:]

    def consensus(merged):
        outbox = jnp.zeros((shards,) + block, F32).at[owner].set(merged)
        inbox = lax.all_to_all(outbox, AXES, split_axis=0, concat_axis=0, tiled=True)
        summed = jnp.einsum("dy,ysh->dsh", delivery, inbox, precision=lax.Precision.HIGHEST)
        z = shrink(summed / share, 1.0 / share)
        back = jnp.einsum("pu,pxa->uxa", delivery, z, precision=lax.Precision.HIGHEST)
        returned = lax.all_to_all(back, AXES, split_axis=0, concat_axis=0, tiled=True)
        return z, returned[owner]

    z, z_local = consensus(x + u)
    x1, r1, u1, _ = solve(True, plan, tile_data, b, x, u, z_local)
    z, z_next = consensus(x1 + u1)
    x2, u2, gap = solve(False, plan, tile_data, x1, u1, z_next, z_local, r1)
    total = lax.psum(jnp.sum(gap, axis=1), AXES)
    primal_gap = jnp.sqrt(total / (shards * local_cols * start_x.shape[1]))
    return flip(x2), flip(u2), flip(z), primal_gap


def solution(mesh):
    split = P(AXES)
    return jax.shard_map(
        on_device, mesh=mesh,
        in_specs=(split, split, split, split, split, P(), split, split, split),
        out_specs=(split, split, split, P()),
        check_vma=False,
    )
```

time: 964 us -> 478 us (0.50); the launches traced: 947 us -> 476 us
  other arithmetic: 181 us -> 10.9 us
  local copies, waits for them, and re-layouts: 188 us -> 42.8 us
  matrix products: 126 us -> 13.3 us
  starting transfers between devices: 148 us -> 38.4 us
  Pallas kernels: 0 us -> 70.1 us
  waiting for transfers between devices: 158 us -> 171 us
  blocking collectives: 140 us -> 128 us
    dot_general x25 -> x4, matrix products: 126 us -> 13.3 us  [the longest x2 9.57 us: consensus(): jnp.einsum('dy,ysh->dsh', delivery, inbox, precision=lax.Precision.HIGHEST)]
    all_to_all x5 -> x4, starting transfers between devices: 148 us -> 38.4 us  [the longest x2 16.6 us: consensus(): lax.all_to_all(back, AXES, split_axis=0, concat_axis=0, tiled=True)]
    scatter-add x21 -> x0, other arithmetic: 98.2 us -> none  [add_group(): return summed.at[landing].add(product * in_use[:, None, None])]
    psum x4 -> x1, blocking collectives: 140 us -> 63.4 us  [on_device(): total = lax.psum(jnp.sum(gap, axis=1), AXES)]
    pallas_call x0 -> x2, Pallas kernels: none -> 70.1 us  [solve(): pl.pallas_call(functools.partial(solve_kernel, first), out_shape=outs, in...]
    all_to_all x0 -> x1, blocking collectives: none -> 64.4 us  [consensus(): lax.all_to_all(outbox, AXES, split_axis=0, concat_axis=0, tiled=True)]
    while x19 -> x0, local copies, waits for them, and re-layouts: 57 us -> none  [tile_pass(): return lax.fori_loop(0, rounds, add_group, initial)]
    gather x23 -> x2, local copies, waits for them, and re-layouts: 60.2 us -> 8.46 us  [consensus(): return (z, returned[owner])]
  transfers between devices with their start and end apart: 5 -> 4, of which waited for: 4 -> 3; matrix products, arithmetic and copies ran while one was open for 10% -> 4% of each run, Pallas kernels for 0% -> 0%
where the time goes in v1:
time: 478 us; the launch traced here: 476 us
  waiting for transfers between devices  171 us (36%)
  blocking collectives  128 us (27%)
  Pallas kernels  70.1 us (15%)
  local copies, waits for them, and re-layouts  42.8 us (9%)
  starting transfers between devices  38.4 us (8%)
  matrix products  13.3 us (3%)
  other arithmetic  10.9 us (2%)
    all_to_all x2, waiting for transfers between devices, consensus(): lax.all_to_all(back, AXES, split_axis=0, concat_axis=0, tiled=True)  115 us
    pallas_call x2, Pallas kernels, solve(): pl.pallas_call(functools.partial(solve_kernel, first), out_shape=outs, in...  70.1 us
    all_to_all x1, blocking collectives, consensus(): lax.all_to_all(outbox, AXES, split_axis=0, concat_axis=0, tiled=True)  64.4 us
    psum x1, blocking collectives, on_device(): total = lax.psum(jnp.sum(gap, axis=1), AXES)  63.4 us
    all_to_all x1, waiting for transfers between devices, consensus(): lax.all_to_all(outbox, AXES, split_axis=0, concat_axis=0, tiled=True)  56.6 us
    scatter x2, local copies, waits for them, and re-layouts, consensus(): outbox = jnp.zeros((shards,) + block, F32).at[owner].set(merged)  17.2 us
    all_to_all x2, starting transfers between devices, consensus(): lax.all_to_all(back, AXES, split_axis=0, concat_axis=0, tiled=True)  16.6 us
    all_to_all x1, starting transfers between devices, on_device(): lax.all_to_all(tags.reshape(shards, 1), AXES, split_axis=0, concat_axis=0...  11.5 us
  transfers between devices with their start and end apart: 4, of which 3 were waited for; matrix products, arithmetic and copies ran while one was open for 4% of the time, Pallas kernels for 0%

profile of v1, /device:TPU:1, one launch (start us, length us, event | category | flops | bytes accessed | tf_op | source)
XLA Modules:
  0.0 476.2 jit_solution(14720156477916743389)
XLA Ops:
  0.6 0.9 select_reduce_fusion
  1.5 0.8 scatter_custom_fusion
  2.3 0.7 copy.33
  3.1 11.5 %all-to-all-start = ((s32[128,1,1]{2,1,0:T(1,128)}), s32[128,1,1]{2,1,0:T(1,128)S(1)}, u32[]{:S(2)}, u32[]{:S(2)}) async-start(s32[128,1,1]{2,1,0:T(1,128)} %copy.33), calls=%async_computation | async-start | bytes 131072 | tf_op jit(solution)/shard_map/all_to_all | solution.py:264
  14.6 2.6 bitcast_add_fusion
  17.2 2.5 broadcast.210.clone
  19.7 8.6 %scatter_fusion = f32[128,64,128]{2,1,0:T(8,128)} fusion(f32[128,64,128]{2,1,0:T(8,128)} %broadcast.210.clone, s32[64]{0:T(128)S(1)} %fusion.27, f32[64,64,128]{2,1,0:T(8,128)S(1)} %bitcast_add_fusion), kind=kCustom, calls=%fused_computation.3 | custom fusion | bytes 6291712 | tf_op jit(solution)/shard_map/scatter | solution.py:272
  28.3 10.3 %all-to-all-start.1 = ((f32[128,64,128]{2,1,0:T(8,128)}), f32[128,64,128]{2,1,0:T(8,128)}, u32[]{:S(2)}, u32[]{:S(2)}) async-start(f32[128,64,128]{2,1,0:T(8,128)} %scatter_fusion), calls=%async_computation.1 | async-start | bytes 8388608 | tf_op jit(solution)/shard_map/all_to_all | solution.py:273
  38.6 2.4 reduce
  41.1 56.6 %all-to-all-done.1 = f32[128,64,128]{2,1,0:T(8,128)} async-done(((f32[128,64,128]{2,1,0:T(8,128)}), f32[128,64,128]{2,1,0:T(8,128)}, u32[]{:S(2)}, u32[]{:S(2)}) %all-to-all-start.1) | async-done | bytes 4194336 | tf_op jit(solution)/shard_map/all_to_all | solution.py:273
  97.7 5.8 %fusion.4 = f32[4,64,128]{2,0,1:T(4,128)S(1)} fusion(f32[128,64,128]{2,1,0:T(8,128)} %all-to-all-done.1, f32[4]{0:T(128)S(1)} %get-tuple-element.48, s32[128]{0:T(128)S(1)} %reduce), kind=kOutput, calls=%fused_computation.9 | convolution fusion | flops 50364928 | bytes 4325904 | tf_op jit(solution)/shard_map/dy,ysh->dsh/dot_general | solution.py:274
  103.5 1.9 fusion.15
  105.3 4.4 copy.35
  109.7 8.1 %all-to-all-start.2 = ((f32[128,64,128]{2,1,0:T(8,128)}), f32[128,64,128]{2,1,0:T(8,128)}, u32[]{:S(2)}, u32[]{:S(2)}) async-start(f32[128,64,128]{2,1,0:T(8,128)} %copy.35), calls=%async_computation.2 | async-start | bytes 8388608 | tf_op jit(solution)/shard_map/all_to_all | solution.py:277
  119.6 1.2 stack.24.refs_0_
  120.8 56.2 %all-to-all-done.2 = f32[128,64,128]{2,1,0:T(8,128)} async-done(((f32[128,64,128]{2,1,0:T(8,128)}), f32[128,64,128]{2,1,0:T(8,128)}, u32[]{:S(2)}, u32[]{:S(2)}) %all-to-all-start.2) | async-done | bytes 4194336 | tf_op jit(solution)/shard_map/all_to_all | solution.py:277
  177.0 4.3 gather_fusion
  181.2 38.8 %solve_first.1 = (f32[64,64,128]{2,1,0:T(8,128)}, f32[64,64,128]{2,1,0:T(8,128)}, f32[64,64,128]{2,1,0:T(8,128)}, f32[64,128]{1,0:T(8,128)}) custom-call(s32[9,64]{1,0:T(8,128)} %stack.24.refs_0_, f32[64,128,128]{2,1,0:T(8,128)} %refs_1_.3, f32[32,64,128]{2,1,0:T(8,128)} %bitcast.72, f32[64,64,128]{2,1,0:T(8,128)} %bitcast.70, f32[64,64,128]{2,1,0:T(8,128)} %bitcast.71, ...), custom_call_target="tpu_custom_call" | custom-call | tf_op jit(solution)/shard_map/solve_first/pallas_call | solution.py:237
  220.1 2.6 add.78
  222.7 2.5 broadcast.210
  225.1 8.6 %scatter_fusion.1 = f32[128,64,128]{2,1,0:T(8,128)} fusion(f32[128,64,128]{2,1,0:T(8,128)} %broadcast.210, s32[64]{0:T(128)S(1)} %fusion.27, f32[64,64,128]{2,1,0:T(8,128)S(1)} %add.78), kind=kCustom, calls=%fused_computation.4 | custom fusion | bytes 6291712 | tf_op jit(solution)/shard_map/scatter | solution.py:272
  233.7 64.4 %all_to_all.29 = f32[128,64,128]{2,1,0:T(8,128)S(1)} all-to-all(f32[128,64,128]{2,1,0:T(8,128)} %scatter_fusion.1), channel_id=1, replica_groups=mesh['dev'=32,'ka'=4] {'dev','ka'}, dimensions={0} | all-to-all | bytes 8388608 | tf_op jit(solution)/shard_map/all_to_all | solution.py:273
  298.1 3.8 bitcast_subtract_fusion
  302.0 1.9 fusion.11
  303.8 4.4 copy.37
  308.2 8.5 %all-to-all-start.4 = ((f32[128,64,128]{2,1,0:T(8,128)}), f32[128,64,128]{2,1,0:T(8,128)}, u32[]{:S(2)}, u32[]{:S(2)}) async-start(f32[128,64,128]{2,1,0:T(8,128)} %copy.37), calls=%async_computation.4 | async-start | bytes 8388608 | tf_op jit(solution)/shard_map/all_to_all | solution.py:277
  316.7 0.7 copy.38
  317.4 58.6 %all-to-all-done.4 = f32[128,64,128]{2,1,0:T(8,128)} async-done(((f32[128,64,128]{2,1,0:T(8,128)}), f32[128,64,128]{2,1,0:T(8,128)}, u32[]{:S(2)}, u32[]{:S(2)}) %all-to-all-start.4) | async-done | bytes 4194336 | tf_op jit(solution)/shard_map/all_to_all | solution.py:277
  376.0 4.2 gather_fusion.1
  380.2 31.3 %solve_next.1 = (f32[64,64,128]{2,1,0:T(8,128)}, f32[64,64,128]{2,1,0:T(8,128)}, f32[64,128]{1,0:T(8,128)}) custom-call(s32[9,64]{1,0:T(8,128)} %stack.24.refs_0_, f32[64,128,128]{2,1,0:T(8,128)} %refs_1_.3, f32[64,64,128]{2,1,0:T(8,128)} %get-tuple-element.10.refs_2_, f32[64,64,128]{2,1,0:T(8,128)} %get-tuple-element.11.refs_3_, ...), custom_call_target="tpu_custom_call" | custom-call | tf_op jit(solution)/shard_map/solve_next/pallas_call | solution.py:237
  411.5 0.9 reduce_sum.118
  412.3 63.4 %psum.7 = f32[64]{0:T(128)S(1)} all-reduce(f32[64]{0:T(128)S(1)} %reduce_sum.118), channel_id=1, replica_groups=mesh['dev'=32,'ka'=4] {'dev','ka'}, use_global_device_ids=true, to_apply=%region_16.17 | all-reduce | flops 64 | bytes 512 | tf_op jit(solution)/shard_map/psum | solution.py:284
  (24 shorter events, 1.7 us)
Async XLA Ops:
  3.1 25.2 %all-to-all-start = ((s32[128,1,1]{2,1,0:T(1,128)}), s32[128,1,1]{2,1,0:T(1,128)S(1)}, u32[]{:S(2)}, u32[]{:S(2)}) async-start(s32[128,1,1]{2,1,0:T(1,128)} %copy.33), calls=%async_computation | async-start | bytes 131072 | tf_op jit(solution)/shard_map/all_to_all | solution.py:264
  28.3 69.4 %all-to-all-start.1 = ((f32[128,64,128]{2,1,0:T(8,128)}), f32[128,64,128]{2,1,0:T(8,128)}, u32[]{:S(2)}, u32[]{:S(2)}) async-start(f32[128,64,128]{2,1,0:T(8,128)} %scatter_fusion), calls=%async_computation.1 | async-start | bytes 8388608 | tf_op jit(solution)/shard_map/all_to_all | solution.py:273
  109.7 8.8 %copy-start = (s32[1,64]{1,0:T(1,128)S(1)}, s32[1,64]{1,0:T(1,128)}, u32[]{:S(2)}) copy-start(s32[1,64]{1,0:T(1,128)} %param.11) | copy-start | bytes 772
  109.7 8.8 %copy-start.1 = (s32[1,64]{1,0:T(1,128)S(1)}, s32[1,64]{1,0:T(1,128)}, u32[]{:S(2)}) copy-start(s32[1,64]{1,0:T(1,128)} %param.10) | copy-start | bytes 772
  109.7 67.3 %all-to-all-start.2 = ((f32[128,64,128]{2,1,0:T(8,128)}), f32[128,64,128]{2,1,0:T(8,128)}, u32[]{:S(2)}, u32[]{:S(2)}) async-start(f32[128,64,128]{2,1,0:T(8,128)} %copy.35), calls=%async_computation.2 | async-start | bytes 8388608 | tf_op jit(solution)/shard_map/all_to_all | solution.py:277
  308.2 67.8 %all-to-all-start.4 = ((f32[128,64,128]{2,1,0:T(8,128)}), f32[128,64,128]{2,1,0:T(8,128)}, u32[]{:S(2)}, u32[]{:S(2)}) async-start(f32[128,64,128]{2,1,0:T(8,128)} %copy.37), calls=%async_computation.4 | async-start | bytes 8388608 | tf_op jit(solution)/shard_map/all_to_all | solution.py:277

commit v2 on v1

--- a/solution.py
+++ b/solution.py
@@ -244,9 +244,282 @@
         name="solve_first" if first else "solve_next",
     )(plan, *arrays)
 
-
-def shrink(amount, cutoff):
-    return amount - jnp.clip(amount, -cutoff, cutoff)
+SIDE = 4
+ORDERS = (("x", "y", "z"), ("y", "z", "x"), ("z", "x", "y"))
+PART_TILES = (3, 3, 2)
+SUB = 8
+PER = 4
+S1, S1F, S2F, S2S, S2D, S3, T3, T2O, T2F, T2D, T1, T1F, SEMS = 0, 8, 9, 10, 11, 12, 16, 20, 21, 22, 23, 31, 32
+
+
+def exchange_plan(owner, slot_tag, shards):
+    y, x, core, z = owner // 32, (owner // 8) % 4, (owner // 4) % 2, owner % 4
+    place = {"x": x, "y": y, "z": z}
+    index = jnp.stack([place[a] * 32 + core * 16 + place[b] * 4 + place[c] for a, b, c in ORDERS])
+    match = index[:, :, None] == jnp.arange(shards, dtype=jnp.int32)[None, None, :]
+    number = jnp.arange(owner.shape[0], dtype=jnp.int32)
+    slot = jnp.sum(jnp.where(match, number[None, :, None], 0), axis=1)
+    tag = jnp.sum(jnp.where(match, slot_tag[None, :, None] + 1, 0), axis=1) - 1
+    index = jnp.pad(index, ((0, 0), (0, shards - owner.shape[0])))
+    return jnp.concatenate([slot, tag, index])
+
+
+def exchange_kernel(table, x_in, u_in, z_local, z_own, *scratch):
+    parts = len(ORDERS)
+    boxes = [scratch[n * parts:(n + 1) * parts] for n in range(12)]
+    mail, in1, fwd1, part2, fwd2, in2, part3, in3, zb2, inbox, sel, zrel = boxes
+    send_sem, recv_sem = scratch[12 * parts:]
+    slots, targets, blk = x_in.shape
+    dev, z = lax.axis_index("dev"), lax.axis_index("ka")
+    core = lax.rem(dev, 2)
+    me = {"x": lax.rem(dev // 2, SIDE), "y": dev // 8, "z": z}
+    way = 1 - 2 * core
+
+    def near(axis, delta, to_core):
+        at = dict(me)
+        at[axis] = lax.rem(me[axis] + delta + SIDE, SIDE)
+        return ((at["y"] * SIDE + at["x"]) * 2 + to_core, at["z"])
+
+    barrier = pltpu.get_barrier_semaphore()
+    friends = [near("x", 0, 1 - core)]
+    for axis in ("x", "y", "z"):
+        friends += [near(axis, 2, core)]
+        friends += [near(axis, delta, c) for delta in (1, -1) for c in (0, 1)]
+    for friend in friends:
+        pl.semaphore_signal(barrier, inc=1, device_id=friend, device_id_type=pl.DeviceIdType.MESH)
+
+    def pack(p):
+        tiles = PART_TILES[p]
+        base = sum(PART_TILES[:p]) * SUB
+        rows = tiles * SUB
+
+        def record(q, _):
+            for i in range(16):
+                slot = table[p, q * 16 + i]
+                tag = table[parts + p, q * 16 + i]
+                where = pl.ds(base, rows)
+                mail[p][q, i * rows:(i + 1) * rows, :] = x_in[slot, where, :] + u_in[slot, where, :]
+                mail[p][q, 16 * rows + i:16 * rows + i + 1, :] = jnp.full((1, blk), tag, jnp.int32).astype(F32)
+            return _
+
+        lax.fori_loop(0, 8, record, 0)
+
+    sends = []
+
+    def copy(p, src, dst, send, recv, device):
+        return pltpu.make_async_remote_copy(
+            src_ref=src, dst_ref=dst, send_sem=send_sem.at[p, send], recv_sem=recv_sem.at[p, recv],
+            device_id=device, device_id_type=pl.DeviceIdType.MESH)
+
+    def go(p, src, dst, send, recv, device):
+        moving = copy(p, src, dst, send, recv, device)
+        moving.start()
+        sends.append(moving)
+
+    def arrive(p, dst, recv):
+        copy(p, dst, dst, 0, recv, near("x", 0, 1 - core)).wait_recv()
+
+    ring = lambda a, delta: lax.rem(me[a] + delta + SIDE, SIDE)
+
+    def scatter_start(p, box, into, relay, base, base_f):
+        a = ORDERS[p][0]
+        go(p, box(ring(a, 2), None), relay, base_f, base_f, near(a, way, core))
+        for delta in (1, 3):
+            for c in (0, 1):
+                go(p, box(ring(a, delta), c), into(delta), base + delta * 2 + c, base + delta * 2 + core, near(a, delta, c))
+        go(p, box(me[a], 1 - core), into(0), base, base + core, near(a, 0, 1 - core))
+
+    def scatter_relay(p, relay, into, base, base_f):
+        a = ORDERS[p][0]
+        arrive(p, relay(None), base_f)
+        for c in (0, 1):
+            go(p, relay(c), into, base + 4 + c, base + 4 + core, near(a, way, c))
+
+    def mail_box(p):
+        return lambda at, c: mail[p].at[pl.ds(at * 2, 2)] if c is None else mail[p].at[at * 2 + c]
+
+    for p in range(parts):
+        pack(p)
+        if p == 0:
+            pl.semaphore_wait(barrier, len(friends))
+        scatter_start(p, mail_box(p), lambda delta: in1[p].at[delta * 2 + core], fwd1[p], S1, S1F)
+    for p in range(parts):
+        relay = lambda c: fwd1[p] if c is None else fwd1[p].at[c]
+        scatter_relay(p, relay, in1[p].at[4 + core], S1, S1F)
+
+    def sources(p):
+        a = ORDERS[p][0]
+        own = lambda rows: mail[p][me[a] * 2 + core, rows, :]
+        found = [(0, core, own)]
+        for delta, c in ((0, 1 - core), (1, 0), (1, 1), (2, 0), (2, 1), (3, 0), (3, 1)):
+            found.append((delta, c, lambda rows, n=delta * 2 + c: in1[p][n, rows, :]))
+        return found
+
+    def combine(p):
+        tiles = PART_TILES[p]
+        rows = tiles * SUB
+        width = PER * rows + SUB
+        found = sources(p)
+
+        def some(a2, _):
+            for a3 in range(SIDE):
+                i = a2 * SIDE + a3
+                tags = [jnp.broadcast_to(read(pl.ds(16 * rows + i, 1)), (SUB, blk)) for _, _, read in found]
+                hits = [[tag == float(k) for tag in tags] for k in range(PER)]
+                for j in range(tiles):
+                    at = pl.multiple_of(i * rows + j * SUB, SUB)
+                    data = [read(pl.ds(at, SUB)) for _, _, read in found]
+                    for k in range(PER):
+                        acc = functools.reduce(
+                            lambda s, n: s + n, [jnp.where(h, v, 0.0) for h, v in zip(hits[k], data)])
+                        start = a3 * width + k * rows + j * SUB
+                        part2[p][a2, start:start + SUB, :] = acc
+                for k in range(PER):
+                    number = functools.reduce(lambda s, n: s + n, [jnp.where(h, 1.0, 0.0) for h in hits[k]])
+                    start = a3 * width + PER * rows + k
+                    part2[p][a2, start:start + 1, :] = number[:1]
+                start = a3 * width + PER * rows + PER
+                part2[p][a2, start:start + SUB - PER, :] = jnp.zeros((SUB - PER, blk), F32)
+            return _
+
+        lax.fori_loop(0, SIDE, some, 0)
+
+    for p in range(parts):
+        for delta, c in ((1, 0), (1, 1), (3, 0), (3, 1), (2, 0), (2, 1), (0, 1 - core)):
+            arrive(p, in1[p].at[delta * 2 + c], S1 + delta * 2 + c)
+        combine(p)
+        b = ORDERS[p][1]
+        go(p, part2[p].at[ring(b, 2)], fwd2[p], S2F, S2F, near(b, way, core))
+        go(p, part2[p].at[ring(b, -way)], in2[p].at[1], S2D, S2D, near(b, -way, core))
+    for p in range(parts):
+        b = ORDERS[p][1]
+        arrive(p, fwd2[p], S2F)
+        at = ring(b, way)
+        part2[p][at] = part2[p][at] + fwd2[p][...]
+        go(p, part2[p].at[at], in2[p].at[0], S2S, S2S, near(b, way, core))
+    for p in range(parts):
+        b, c3 = ORDERS[p][1], ORDERS[p][2]
+        width = PER * PART_TILES[p] * SUB + SUB
+        arrive(p, in2[p].at[1], S2D)
+        arrive(p, in2[p].at[0], S2S)
+        whole = part2[p][me[b]] + in2[p][0] + in2[p][1]
+        for a3 in range(SIDE):
+            part3[p][a3] = whole[a3 * width:(a3 + 1) * width]
+        for delta in (1, 2, 3):
+            go(p, part3[p].at[ring(c3, delta)], in3[p].at[delta - 1], S3 + delta, S3 + delta, near(c3, delta, core))
+    for p in range(parts):
+        b, c3 = ORDERS[p][1], ORDERS[p][2]
+        rows = PART_TILES[p] * SUB
+        base = sum(PART_TILES[:p]) * SUB
+        for delta in (1, 2, 3):
+            arrive(p, in3[p].at[delta - 1], S3 + delta)
+        whole = ((part3[p][me[c3]] + in3[p][0]) + in3[p][1]) + in3[p][2]
+        for k in range(PER):
+            number = whole[PER * rows + k:PER * rows + k + 1]
+            share = jnp.maximum(number, 1.0)
+            value = whole[k * rows:(k + 1) * rows] / share
+            cut = jnp.broadcast_to(1.0 / share, value.shape)
+            value = value - jnp.minimum(jnp.maximum(value, -cut), cut)
+            z_own[k, base:base + rows, :] = value
+            zb2[p][me[b], me[c3], k * rows:(k + 1) * rows, :] = value
+        own = zb2[p].at[me[b], me[c3]]
+        for delta in (1, 2, 3):
+            go(p, own, own, T3 + delta, T3 + delta, near(c3, delta, core))
+    for p in range(parts):
+        b, c3 = ORDERS[p][1], ORDERS[p][2]
+        for delta in (1, 2, 3):
+            arrive(p, zb2[p].at[me[b], ring(c3, -delta)], T3 + delta)
+        own = zb2[p].at[me[b]]
+        go(p, own, own, T2O, T2O, near(b, way, core))
+        go(p, own, own, T2D, T2D, near(b, -way, core))
+    for p in range(parts):
+        b = ORDERS[p][1]
+        passing = zb2[p].at[ring(b, -way)]
+        arrive(p, passing, T2O)
+        go(p, passing, passing, T2F, T2F, near(b, way, core))
+
+    def select(p):
+        tiles = PART_TILES[p]
+        rows = tiles * SUB
+        a = ORDERS[p][0]
+        found = sources(p)
+
+        def some(a2, _):
+            for a3 in range(SIDE):
+                i = a2 * SIDE + a3
+                blocks = [zb2[p][a2, a3, n * SUB:(n + 1) * SUB, :] for n in range(PER * tiles)]
+                for number, (delta, c, read) in enumerate(found):
+                    tag = jnp.broadcast_to(read(pl.ds(16 * rows + i, 1)), (SUB, blk))
+                    hit = [tag == float(k) for k in range(PER - 1)]
+                    for j in range(tiles):
+                        value = blocks[(PER - 1) * tiles + j]
+                        for k in range(PER - 1):
+                            value = jnp.where(hit[k], blocks[k * tiles + j], value)
+                        if number == 0:
+                            inbox[p][(me[a] * 2 + core) * 16 + i, j * SUB:(j + 1) * SUB, :] = value
+                        else:
+                            sel[p][(ring(a, -delta) * 2 + c) * 16 + i, j * SUB:(j + 1) * SUB, :] = value
+            return _
+
+        lax.fori_loop(0, SIDE, some, 0)
+
+    for p in range(parts):
+        a, b = ORDERS[p][0], ORDERS[p][1]
+        arrive(p, zb2[p].at[ring(b, way)], T2D)
+        arrive(p, zb2[p].at[ring(b, 2)], T2F)
+        select(p)
+        box = lambda at, c: sel[p].at[pl.ds(at * 32, 32)] if c is None else sel[p].at[pl.ds((at * 2 + c) * 16, 16)]
+        mine = inbox[p].at[pl.ds((me[a] * 2 + core) * 16, 16)]
+        scatter_start(p, box, lambda delta: mine, zrel[p], T1, T1F)
+    for p in range(parts):
+        a = ORDERS[p][0]
+        relay = lambda c: zrel[p] if c is None else zrel[p].at[pl.ds(c * 16, 16)]
+        scatter_relay(p, relay, inbox[p].at[pl.ds((ring(a, -way) * 2 + core) * 16, 16)], T1, T1F)
+
+    def unpack(p):
+        rows = PART_TILES[p] * SUB
+        base = sum(PART_TILES[:p]) * SUB
+
+        def group(g, _):
+            for n in range(8):
+                c = g * 8 + n
+                z_local[c, base:base + rows, :] = inbox[p][table[2 * parts + p, c]]
+            return _
+
+        lax.fori_loop(0, slots // 8, group, 0)
+
+    for p in range(parts):
+        a = ORDERS[p][0]
+        for delta, c in ((1, 0), (1, 1), (3, 0), (3, 1), (2, 0), (2, 1), (0, 1 - core)):
+            arrive(p, inbox[p].at[pl.ds((ring(a, -delta) * 2 + c) * 16, 16)], T1 + delta * 2 + c)
+        unpack(p)
+    for moving in sends:
+        moving.wait_send()
+
+
+def exchange(number, table, x, u):
+    slots, targets, blk = x.shape
+    each = lambda shape: [pltpu.VMEM(shape(t * SUB), F32) for t in PART_TILES]
+    scratch = (
+        each(lambda r: (8, 16 * r + 16, blk)) + each(lambda r: (8, 16 * r + 16, blk))
+        + each(lambda r: (2, 16 * r + 16, blk)) + each(lambda r: (SIDE, SIDE * (PER * r + SUB), blk))
+        + each(lambda r: (SIDE * (PER * r + SUB), blk)) + each(lambda r: (2, SIDE * (PER * r + SUB), blk))
+        + each(lambda r: (SIDE, PER * r + SUB, blk)) + each(lambda r: (3, PER * r + SUB, blk))
+        + each(lambda r: (SIDE, SIDE, PER * r, blk)) + each(lambda r: (128, r, blk))
+        + each(lambda r: (128, r, blk)) + each(lambda r: (32, r, blk))
+        + [pltpu.SemaphoreType.DMA((len(ORDERS), SEMS)), pltpu.SemaphoreType.DMA((len(ORDERS), SEMS))]
+    )
+    whole = pl.BlockSpec(memory_space=pltpu.VMEM)
+    return pl.pallas_call(
+        exchange_kernel,
+        out_shape=(jax.ShapeDtypeStruct(x.shape, F32), jax.ShapeDtypeStruct((PER, targets, blk), F32)),
+        in_specs=[pl.BlockSpec(memory_space=pltpu.SMEM), whole, whole],
+        out_specs=(whole, whole),
+        scratch_shapes=scratch,
+        compiler_params=pltpu.CompilerParams(
+            collective_id=number, has_side_effects=True, vmem_limit_bytes=60 * 1024 * 1024),
+        name="exchange",
+    )(table, x, u)
 
 
 def on_device(tile_data, tile_row, tile_col, tile_count, touched, owner_map, observed, start_x, start_u):
@@ -260,26 +533,12 @@
     position = jnp.sum(matches * owner_map[None, :], axis=1)
     owner = position // col_dev
     local_slot = position - owner * col_dev
-    tags = jnp.full((shards,), -1, jnp.int32).at[owner].set(local_slot)
-    arrived = lax.all_to_all(tags.reshape(shards, 1), AXES, split_axis=0, concat_axis=0, tiled=True).reshape(-1)
-    delivery = (arrived[None, :] == jnp.arange(col_dev, dtype=jnp.int32)[:, None]).astype(F32)
-    share = jnp.maximum(jnp.sum(delivery, axis=1), 1.0)[:, None, None]
+    table = exchange_plan(owner, local_slot, shards)
     flip = lambda a: jnp.swapaxes(a, 1, 2)
     x, u, b = flip(start_x), flip(start_u), flip(observed)
-    block = x.shape[1:]
-
-    def consensus(merged):
-        outbox = jnp.zeros((shards,) + block, F32).at[owner].set(merged)
-        inbox = lax.all_to_all(outbox, AXES, split_axis=0, concat_axis=0, tiled=True)
-        summed = jnp.einsum("dy,ysh->dsh", delivery, inbox, precision=lax.Precision.HIGHEST)
-        z = shrink(summed / share, 1.0 / share)
-        back = jnp.einsum("pu,pxa->uxa", delivery, z, precision=lax.Precision.HIGHEST)
-        returned = lax.all_to_all(back, AXES, split_axis=0, concat_axis=0, tiled=True)
-        return z, returned[owner]
-
-    z, z_local = consensus(x + u)
+    z_local, z = exchange(0, table, x, u)
     x1, r1, u1, _ = solve(True, plan, tile_data, b, x, u, z_local)
-    z, z_next = consensus(x1 + u1)
+    z_next, z = exchange(1, table, x1, u1)
     x2, u2, gap = solve(False, plan, tile_data, x1, u1, z_next, z_local, r1)
     total = lax.psum(jnp.sum(gap, axis=1), AXES)
     primal_gap = jnp.sqrt(total / (shards * local_cols * start_x.shape[1]))

time: 478 us -> 302 us (0.63)
  waiting for transfers between devices: 171 us -> 0 us
  Pallas kernels: 70.1 us -> 230 us
  blocking collectives: 128 us -> 62.4 us
  local copies, waits for them, and re-layouts: 42.8 us -> 1.95 us
  starting transfers between devices: 38.4 us -> 0 us
  matrix products: 13.3 us -> 0 us
  other arithmetic: 10.9 us -> 5.94 us
    all_to_all x4 -> x0, waiting for transfers between devices: 171 us -> none  [the longest x2 115 us: consensus(): lax.all_to_all(back, AXES, split_axis=0, concat_axis=0, tiled=True)]
    pallas_call x0 -> x2, Pallas kernels: none -> 159 us  [exchange(): pl.pallas_call(exchange_kernel, out_shape=(jax.ShapeDtypeStruct(x.shape,...]
    all_to_all x1 -> x0, blocking collectives: 64.4 us -> none  [consensus(): lax.all_to_all(outbox, AXES, split_axis=0, concat_axis=0, tiled=True)]
    all_to_all x4 -> x0, starting transfers between devices: 38.4 us -> none  [the longest x2 16.6 us: consensus(): lax.all_to_all(back, AXES, split_axis=0, concat_axis=0, tiled=True)]
    scatter x3 -> x0, local copies, waits for them, and re-layouts: 17.9 us -> none  [the longest x2 17.2 us: consensus(): outbox = jnp.zeros((shards,) + block, F32).at[owner].set(merged)]
    dot_general x4 -> x0, matrix products: 13.3 us -> none  [the longest x2 9.57 us: consensus(): jnp.einsum('dy,ysh->dsh', delivery, inbox, precision=lax.Precision.HIGHEST)]
    dot_general x2 -> x0, local copies, waits for them, and re-layouts: 8.8 us -> none  [consensus(): jnp.einsum('pu,pxa->uxa', delivery, z, precision=lax.Precision.HIGHEST)]
    gather x2 -> x0, local copies, waits for them, and re-layouts: 8.46 us -> none  [consensus(): return (z, returned[owner])]
  transfers between devices with their start and end apart: 4 -> 0, of which waited for: 3 -> 0; matrix products, arithmetic and copies ran while one was open for 4% -> 0% of each run, Pallas kernels for 0% -> 0%
where the time goes in v2:
time: 302 us; the launch traced here: 301 us
  Pallas kernels  230 us (76%)
  blocking collectives  62.4 us (21%)
  other arithmetic  5.94 us (2%)
    pallas_call x2, Pallas kernels, exchange(): pl.pallas_call(exchange_kernel, out_shape=(jax.ShapeDtypeStruct(x.shape,...  159 us
    pallas_call x2, Pallas kernels, solve(): pl.pallas_call(functools.partial(solve_kernel, first), out_shape=outs, in...  70.2 us
    psum x1, blocking collectives, on_device(): total = lax.psum(jnp.sum(gap, axis=1), AXES)  62.4 us

profile of v2, /device:TPU:1, one launch (start us, length us, event | category | flops | bytes accessed | tf_op | source)
XLA Modules:
  0.0 301.2 jit_solution(1259107554810968571)
XLA Ops:
  1.3 0.9 select_reduce_fusion
  2.2 0.7 iota_add_fusion
  2.9 0.7 add_bitcast_fusion.1
  3.6 0.2 convert_reduce_fusion
  3.8 0.2 convert_reduce_fusion.1
  3.9 0.9 select_reduce_fusion.6
  4.8 0.2 select_reduce_fusion.3
  5.0 0.1 compare_convert_fusion
  5.1 0.1 slice_bitcast_fusion.1
  5.2 0.1 and_convert_fusion
  5.2 1.2 stack.30.refs_0_
  6.4 0.1 select_reduce_fusion.2
  6.6 0.6 pad_add_fusion.table
  7.2 82.4 %exchange.2 = (f32[64,64,128]{2,1,0:T(8,128)}, f32[4,64,128]{2,1,0:T(8,128)}) custom-call(s32[9,128]{1,0:T(8,128)} %pad_add_fusion.table, f32[64,64,128]{2,1,0:T(8,128)} %bitcast.101, f32[64,64,128]{2,1,0:T(8,128)} %bitcast.103), custom_call_target="tpu_custom_call" | custom-call | tf_op jit(solution)/shard_map/exchange/pallas_call | solution.py:513
  89.6 38.8 %solve_first.1 = (f32[64,64,128]{2,1,0:T(8,128)}, f32[64,64,128]{2,1,0:T(8,128)}, f32[64,64,128]{2,1,0:T(8,128)}, f32[64,128]{1,0:T(8,128)}) custom-call(s32[9,64]{1,0:T(8,128)} %stack.30.refs_0_, f32[64,128,128]{2,1,0:T(8,128)} %refs_1_.3, f32[32,64,128]{2,1,0:T(8,128)} %bitcast.105, f32[64,64,128]{2,1,0:T(8,128)} %bitcast.102, f32[64,64,128]{2,1,0:T(8,128)} %bitcast.104, ...), custom_call_target="tpu_custom_call" | custom-call | tf_op jit(solution)/shard_map/solve_first/pallas_call | solution.py:237
  128.4 77.1 %exchange.3 = (f32[64,64,128]{2,1,0:T(8,128)}, f32[4,64,128]{2,1,0:T(8,128)}) custom-call(s32[9,128]{1,0:T(8,128)} %pad_add_fusion.table, f32[64,64,128]{2,1,0:T(8,128)} %get-tuple-element.14.x_in.refs_2_, f32[64,64,128]{2,1,0:T(8,128)} %get-tuple-element.15.u_in.refs_3_), custom_call_target="tpu_custom_call" | custom-call | tf_op jit(solution)/shard_map/exchange/pallas_call | solution.py:513
  205.5 0.0 copy-start
  205.5 31.3 %solve_next.1 = (f32[64,64,128]{2,1,0:T(8,128)}, f32[64,64,128]{2,1,0:T(8,128)}, f32[64,128]{1,0:T(8,128)}) custom-call(s32[9,64]{1,0:T(8,128)} %stack.30.refs_0_, f32[64,128,128]{2,1,0:T(8,128)} %refs_1_.3, f32[64,64,128]{2,1,0:T(8,128)} %get-tuple-element.14.x_in.refs_2_, f32[64,64,128]{2,1,0:T(8,128)} %get-tuple-element.15.u_in.refs_3_, ...), custom_call_target="tpu_custom_call" | custom-call | tf_op jit(solution)/shard_map/solve_next/pallas_call | solution.py:237
  236.8 0.9 reduce_sum.128
  237.7 62.4 %psum.7 = f32[64]{0:T(128)S(1)} all-reduce(f32[64]{0:T(128)S(1)} %reduce_sum.128), channel_id=1, replica_groups=mesh['dev'=32,'ka'=4] {'dev','ka'}, use_global_device_ids=true, to_apply=%region_14.15 | all-reduce | flops 64 | bytes 512 | tf_op jit(solution)/shard_map/psum | solution.py:543
  300.1 0.5 multiply_sqrt_fusion
  300.6 0.0 copy-done
  300.6 0.7 copy.15
  (8 shorter events, 0.1 us)
Async XLA Ops:
  205.5 95.1 %copy-start = (f32[4,64,128]{2,1,0:T(8,128)S(1)}, f32[4,64,128]{2,1,0:T(8,128)}, u32[]{:S(2)}) copy-start(f32[4,64,128]{2,1,0:T(8,128)} %get-tuple-element.20) | copy-start | bytes 393220

commit v3 on v1

v3 whole, which is shorter than its diff:
```python
import functools

import jax
import jax.numpy as jnp
from jax import lax
from jax.experimental import pallas as pl
from jax.experimental.pallas import tpu as pltpu
from jax.sharding import PartitionSpec as P

ITERS = 2
CG_STEPS = 4
GROUP = 16
AXES = ("dev", "ka")
F32 = jnp.float32
BF16 = jnp.bfloat16
MESH = pl.DeviceIdType.MESH

SIDE = 4
SUB = 8
PER = 4
ORDERS = (("x", "y", "z"), ("y", "z", "x"), ("z", "x", "y"))
SETS = ((3, 3, 2),)
S1, S1F, S2F, S2S, S2D, S3, T3, T2O, T2F, T2D, T1, T1F, SEMS = 0, 8, 9, 10, 11, 12, 16, 20, 21, 22, 23, 31, 32
BOXES = 12


def fold(values):
    return functools.reduce(lambda s, n: s + n, values)


def split_store(ref, index, value):
    rows = value.shape[0]
    high = value.astype(BF16)
    low = (value - high.astype(F32)).astype(BF16)
    ref[index, :rows, :] = high
    ref[index, rows:, :] = low


def join(wide, rows, cols):
    return (wide[:rows, :cols] + wide[:rows, cols:]) + wide[rows:, :cols]


def total_of(value):
    return jnp.sum(value, axis=1, keepdims=True)


def tile_plan(rows, cols, count):
    tiles = rows.shape[0]
    place = jnp.arange(tiles, dtype=jnp.int32)
    used = place < count

    def order(key):
        code = jnp.where(used, key, tiles) * tiles + place
        rank = jnp.sum((code[None, :] < code[:, None]).astype(jnp.int32), axis=1)
        pick = rank[None, :] == place[:, None]
        return rank, pick

    def take(pick, values):
        return jnp.sum(jnp.where(pick, values[None, :], 0), axis=1)

    row_key = jnp.where(used, rows, tiles)
    col_key = jnp.where(used, cols, tiles)
    rank_f, pick_f = order(rows)
    rank_b, pick_b = order(cols)
    row_sorted = take(pick_f, row_key)
    col_sorted = take(pick_b, col_key)
    before = lambda s: jnp.concatenate([jnp.full((1,), -1, jnp.int32), s[:-1]])
    after = lambda s: jnp.concatenate([s[1:], jnp.full((1,), -1, jnp.int32)])
    keep_f = (row_sorted == before(row_sorted)).astype(jnp.int32)
    keep_b = (col_sorted == before(col_sorted)).astype(jnp.int32)
    ends_f = ((row_sorted != after(row_sorted)) & (row_sorted < tiles)).astype(jnp.int32)
    last_of_row = jnp.max(jnp.where(row_key[:, None] == row_key[None, :], rank_f[None, :], 0), axis=1)
    column = jnp.arange(tiles, dtype=jnp.int32)
    last_of_col = jnp.max(jnp.where(col_key[None, :] == column[:, None], rank_b[None, :] + 1, 0), axis=1)
    last_of_col = jnp.where(last_of_col == 0, tiles, last_of_col - 1)
    return jnp.stack([
        take(pick_f, place), take(pick_f, cols), keep_f, ends_f, jnp.minimum(row_sorted, 31),
        take(pick_b, place), take(pick_b, last_of_row), keep_b, last_of_col,
    ])

def exchange_plan(owner, slot_tag, shards):
    y, x, core, z = owner // 32, (owner // 8) % 4, (owner // 4) % 2, owner % 4
    place = {"x": x, "y": y, "z": z}
    index = jnp.stack([place[a] * 32 + core * 16 + place[b] * 4 + place[c] for a, b, c in ORDERS])
    match = index[:, :, None] == jnp.arange(shards, dtype=jnp.int32)[None, None, :]
    number = jnp.arange(owner.shape[0], dtype=jnp.int32)
    slot = jnp.sum(jnp.where(match, number[None, :, None], 0), axis=1)
    tag = jnp.sum(jnp.where(match, slot_tag[None, :, None] + 1, 0), axis=1) - 1
    index = jnp.pad(index, ((0, 0), (0, shards - owner.shape[0])))
    return jnp.concatenate([slot, tag, index])


def loop(count, step, body, *init):
    def group(g, carry):
        for n in range(step):
            carry = body(g * step + n, *carry)
        return carry

    return lax.fori_loop(0, count // step, group, init)


def near_device(me, axis, delta, to_core):
    at = dict(me)
    at[axis] = lax.rem(me[axis] + delta + SIDE, SIDE)
    return ((at["y"] * SIDE + at["x"]) * 2 + to_core, at["z"])


class Place:
    def __init__(self):
        dev, z = lax.axis_index("dev"), lax.axis_index("ka")
        self.core = lax.rem(dev, 2)
        self.me = {"x": lax.rem(dev // 2, SIDE), "y": dev // 8, "z": z}
        self.way = 1 - 2 * self.core
        self.partner = (dev + 1 - 2 * self.core, z)

    def near(self, axis, delta, to_core=None):
        return near_device(self.me, axis, delta, self.core if to_core is None else to_core)

    def ring(self, axis, delta):
        return lax.rem(self.me[axis] + delta + SIDE, SIDE)


class Exchange:
    def __init__(self, at, table, tiles, base, boxes, send_sem, recv_sem):
        self.at, self.table, self.tiles = at, table, tiles
        self.base = [(base + sum(tiles[:p])) * SUB for p in range(len(tiles))]
        (self.mail, self.in1, self.fwd1, self.part2, self.fwd2, self.in2, self.part3, self.in3,
         self.zb2, self.inbox, self.sel, self.zrel) = boxes
        self.send_sem, self.recv_sem = send_sem, recv_sem
        self.sends = []
        self.parts = range(len(tiles))

    def copy(self, p, src, dst, send, recv, device):
        return pltpu.make_async_remote_copy(
            src_ref=src, dst_ref=dst, send_sem=self.send_sem.at[p, send], recv_sem=self.recv_sem.at[p, recv],
            device_id=device, device_id_type=MESH)

    def go(self, p, src, dst, send, recv, device):
        moving = self.copy(p, src, dst, send, recv, device)
        moving.start()
        self.sends.append(moving)

    def arrive(self, p, dst, recv):
        self.copy(p, dst, dst, 0, recv, self.at.partner).wait_recv()

    def sent(self):
        for moving in self.sends:
            moving.wait_send()
        self.sends = []

    def pack(self, p, x, u):
        rows = self.tiles[p] * SUB
        where = pl.ds(self.base[p], rows)
        table, parts, mail = self.table, len(ORDERS), self.mail[p]

        def record(q, _):
            for i in range(16):
                slot = table[p, q * 16 + i]
                tag = table[parts + p, q * 16 + i]
                mail[q, i * rows:(i + 1) * rows, :] = x[slot, where, :] + u[slot, where, :]
                mail[q, 16 * rows + i:16 * rows + i + 1, :] = jnp.full((1, x.shape[2]), tag, jnp.int32).astype(F32)
            return (_,)

        loop(8, 1, record, 0)

    def scatter(self, p, box, into, relay, base, base_f):
        at, a, core = self.at, ORDERS[p][0], self.at.core
        self.go(p, box(at.ring(a, 2), None), relay, base_f, base_f, at.near(a, at.way))
        for delta in (1, 3):
            for c in (0, 1):
                self.go(p, box(at.ring(a, delta), c), into(delta), base + delta * 2 + c,
                        base + delta * 2 + core, at.near(a, delta, c))
        self.go(p, box(at.me[a], 1 - core), into(0), base, base + core, at.partner)

    def relay(self, p, relay, into, base, base_f):
        at, a = self.at, ORDERS[p][0]
        self.arrive(p, relay(None), base_f)
        for c in (0, 1):
            self.go(p, relay(c), into, base + 4 + c, base + 4 + at.core, at.near(a, at.way, c))

    def start(self, p, x, u):
        self.pack(p, x, u)

        def box(place, c):
            return self.mail[p].at[pl.ds(place * 2, 2)] if c is None else self.mail[p].at[place * 2 + c]

        return lambda: self.scatter(
            p, box, lambda delta: self.in1[p].at[delta * 2 + self.at.core], self.fwd1[p], S1, S1F)

    def pass_on(self):
        for p in self.parts:
            fwd = self.fwd1[p]
            self.relay(p, lambda c: fwd if c is None else fwd.at[c], self.in1[p].at[4 + self.at.core], S1, S1F)

    def sources(self, p):
        at, a = self.at, ORDERS[p][0]
        mail, in1 = self.mail[p], self.in1[p]
        found = [(0, at.core, lambda rows: mail[at.me[a] * 2 + at.core, rows, :])]
        for delta, c in ((0, 1 - at.core), (1, 0), (1, 1), (2, 0), (2, 1), (3, 0), (3, 1)):
            found.append((delta, c, lambda rows, n=delta * 2 + c: in1[n, rows, :]))
        return found

    def others(self):
        return ((1, 0), (1, 1), (3, 0), (3, 1), (0, 1 - self.at.core), (2, 0), (2, 1))

    def combine(self, p):
        tiles = self.tiles[p]
        rows = tiles * SUB
        width = PER * rows + SUB
        found = self.sources(p)
        part2 = self.part2[p]
        blk = part2.shape[2]

        def some(a2, _):
            for a3 in range(SIDE):
                i = a2 * SIDE + a3
                tags = [jnp.broadcast_to(read(pl.ds(16 * rows + i, 1)), (SUB, blk)) for _, _, read in found]
                hits = [[tag == float(k) for tag in tags] for k in range(PER)]
                for j in range(tiles):
                    place = pl.multiple_of(i * rows + j * SUB, SUB)
                    data = [read(pl.ds(place, SUB)) for _, _, read in found]
                    for k in range(PER):
                        start = a3 * width + k * rows + j * SUB
                        part2[a2, start:start + SUB, :] = fold(
                            [jnp.where(h, v, 0.0) for h, v in zip(hits[k], data)])
                for k in range(PER):
                    start = a3 * width + PER * rows + k
                    part2[a2, start:start + 1, :] = fold([jnp.where(h, 1.0, 0.0) for h in hits[k]])[:1]
                start = a3 * width + PER * rows + PER
                part2[a2, start:start + SUB - PER, :] = jnp.zeros((SUB - PER, blk), F32)
            return (_,)

        loop(SIDE, 1, some, 0)

    def reduce_first(self):
        at = self.at
        for p in self.parts:
            b = ORDERS[p][1]
            for delta, c in self.others():
                self.arrive(p, self.in1[p].at[delta * 2 + c], S1 + delta * 2 + c)
            self.combine(p)
            self.go(p, self.part2[p].at[at.ring(b, 2)], self.fwd2[p], S2F, S2F, at.near(b, at.way))
            self.go(p, self.part2[p].at[at.ring(b, -at.way)], self.in2[p].at[1], S2D, S2D, at.near(b, -at.way))

    def reduce_second(self):
        at = self.at
        for p in self.parts:
            b = ORDERS[p][1]
            self.arrive(p, self.fwd2[p], S2F)
            to = at.ring(b, at.way)
            self.part2[p][to] = self.part2[p][to] + self.fwd2[p][...]
            self.go(p, self.part2[p].at[to], self.in2[p].at[0], S2S, S2S, at.near(b, at.way))

    def reduce_third(self):
        at = self.at
        for p in self.parts:
            b, d = ORDERS[p][1], ORDERS[p][2]
            width = PER * self.tiles[p] * SUB + SUB
            self.arrive(p, self.in2[p].at[1], S2D)
            self.arrive(p, self.in2[p].at[0], S2S)
            whole = self.part2[p][at.me[b]] + self.in2[p][0] + self.in2[p][1]
            for a3 in range(SIDE):
                self.part3[p][a3] = whole[a3 * width:(a3 + 1) * width]
            for delta in (2, 1, 3):
                self.go(p, self.part3[p].at[at.ring(d, delta)], self.in3[p].at[delta - 1],
                        S3 + delta, S3 + delta, at.near(d, delta))

    def agree(self, z_own):
        at = self.at
        for p in self.parts:
            b, d = ORDERS[p][1], ORDERS[p][2]
            rows, base = self.tiles[p] * SUB, self.base[p]
            for delta in (1, 3, 2):
                self.arrive(p, self.in3[p].at[delta - 1], S3 + delta)
            whole = ((self.part3[p][at.me[d]] + self.in3[p][0]) + self.in3[p][1]) + self.in3[p][2]
            for k in range(PER):
                number = whole[PER * rows + k:PER * rows + k + 1]
                share = jnp.maximum(number, 1.0)
                value = whole[k * rows:(k + 1) * rows] / share
                cut = jnp.broadcast_to(1.0 / share, value.shape)
                value = value - jnp.minimum(jnp.maximum(value, -cut), cut)
                z_own[k, base:base + rows, :] = value
                self.zb2[p][at.me[b], at.me[d], k * rows:(k + 1) * rows, :] = value
            own = self.zb2[p].at[at.me[b], at.me[d]]
            for delta in (2, 1, 3):
                self.go(p, own, own, T3 + delta, T3 + delta, at.near(d, delta))

    def spread_first(self):
        at = self.at
        for p in self.parts:
            b, d = ORDERS[p][1], ORDERS[p][2]
            for delta in (1, 3, 2):
                self.arrive(p, self.zb2[p].at[at.me[b], at.ring(d, -delta)], T3 + delta)
            own = self.zb2[p].at[at.me[b]]
            self.go(p, own, own, T2O, T2O, at.near(b, at.way))
            self.go(p, own, own, T2D, T2D, at.near(b, -at.way))

    def spread_second(self):
        at = self.at
        for p in self.parts:
            b = ORDERS[p][1]
            passing = self.zb2[p].at[at.ring(b, -at.way)]
            self.arrive(p, passing, T2O)
            self.go(p, passing, passing, T2F, T2F, at.near(b, at.way))

    def select(self, p):
        at = self.at
        tiles = self.tiles[p]
        rows = tiles * SUB
        a = ORDERS[p][0]
        found = self.sources(p)
        zb2, inbox, sel = self.zb2[p], self.inbox[p], self.sel[p]

        def some(a2, _):
            for a3 in range(SIDE):
                i = a2 * SIDE + a3
                blocks = [zb2[a2, a3, n * SUB:(n + 1) * SUB, :] for n in range(PER * tiles)]
                for number, (delta, c, read) in enumerate(found):
                    tag = jnp.broadcast_to(read(pl.ds(16 * rows + i, 1)), blocks[0].shape)
                    hit = [tag == float(k) for k in range(PER - 1)]
                    for j in range(tiles):
                        value = blocks[(PER - 1) * tiles + j]
                        for k in range(PER - 1):
                            value = jnp.where(hit[k], blocks[k * tiles + j], value)
                        place = (at.ring(a, -delta) * 2 + c) * 16 + i
                        (sel if number else inbox)[place, j * SUB:(j + 1) * SUB, :] = value
            return (_,)

        loop(SIDE, 1, some, 0)

    def give_back(self):
        at = self.at
        self.sent()
        for p in self.parts:
            a, b = ORDERS[p][0], ORDERS[p][1]
            self.arrive(p, self.zb2[p].at[at.ring(b, at.way)], T2D)
            self.arrive(p, self.zb2[p].at[at.ring(b, 2)], T2F)
            self.select(p)
            sel = self.sel[p]

            def box(place, c):
                return sel.at[pl.ds(place * 32, 32)] if c is None else sel.at[pl.ds((place * 2 + c) * 16, 16)]

            mine = self.inbox[p].at[pl.ds((at.me[a] * 2 + at.core) * 16, 16)]
            self.scatter(p, box, lambda delta: mine, self.zrel[p], T1, T1F)

    def give_on(self):
        at = self.at
        for p in self.parts:
            zrel, a = self.zrel[p], ORDERS[p][0]
            self.relay(p, lambda c: zrel if c is None else zrel.at[pl.ds(c * 16, 16)],
                       self.inbox[p].at[pl.ds((at.ring(a, -at.way) * 2 + at.core) * 16, 16)], T1, T1F)

    def finish(self):
        at = self.at
        for p in self.parts:
            a = ORDERS[p][0]
            for delta, c in self.others():
                self.arrive(p, self.inbox[p].at[pl.ds((at.ring(a, -delta) * 2 + c) * 16, 16)], T1 + delta * 2 + c)
        self.sent()

    def read(self, c):
        found = [self.inbox[p][self.table[2 * len(ORDERS) + p, c]] for p in self.parts]
        return jnp.concatenate(found, axis=0)


class Solver:
    def __init__(self, plan, tiles_hl, x, u, r, p, p_hl, image_hl, back, z_before):
        self.plan, self.tiles_hl = plan, tiles_hl
        self.x, self.u, self.r, self.p = x, u, r, p
        self.p_hl, self.image_hl, self.back, self.z_before = p_hl, image_hl, back, z_before
        self.slots, self.blk = p_hl.shape[0], p_hl.shape[2]
        self.targets = p_hl.shape[1] // 2
        self.zero = jnp.zeros((self.targets, self.blk), F32)

    def forward(self, observed=None, square=False):
        plan, targets, blk = self.plan, self.targets, self.blk

        def tile_step(k, acc, total):
            wide = lax.dot_general(
                self.p_hl[plan[1, k]], self.tiles_hl[plan[0, k]], (((1,), (1,)), ((), ())),
                preferred_element_type=F32)
            acc = jnp.where(plan[2, k] > 0, acc, 0.0) + join(wide, targets, blk)
            if square:
                total = total + jnp.where(plan[3, k] > 0, acc * acc, 0.0)
            elif observed is not None:
                split_store(self.image_hl, k, observed[plan[4, k]] - acc)
            else:
                split_store(self.image_hl, k, acc)
            return acc, total

        return loop(self.slots, GROUP, tile_step, self.zero, self.zero)[1]

    def backward(self):
        plan, targets, blk = self.plan, self.targets, self.blk

        def tile_step(k, acc):
            both = self.tiles_hl[plan[5, k]]
            weights = jnp.concatenate([both[:blk], both[blk:]], axis=1)
            wide = jnp.dot(self.image_hl[plan[6, k]], weights, preferred_element_type=F32)
            acc = jnp.where(plan[7, k] > 0, acc, 0.0) + join(wide, targets, blk)
            self.back[k] = acc
            return (acc,)

        loop(self.slots, GROUP, tile_step, self.zero)

    def load_x(self):
        def one(c, _):
            split_store(self.p_hl, c, self.x[c])
            return (_,)

        loop(self.slots, 4, one, 0)

    def begin(self, first, z_of):
        def one(c, rr, gap):
            z, x, u = z_of(c), self.x[c], self.u[c]
            diff = x - z
            u_new = u + diff
            self.u[c] = u_new
            if first:
                r = self.back[self.plan[8, c]] + (z - u_new) - x
                self.z_before[c] = z
            else:
                r = self.r[c] + ((z - u_new) - (self.z_before[c] - u))
            self.r[c] = r
            self.p[c] = r
            split_store(self.p_hl, c, r)
            return rr + r * r, gap + diff * diff

        rr, gap = loop(self.slots, 4, one, self.zero, self.zero)
        self.rr = total_of(rr)
        return gap

    def step(self, last):
        p, r, x, back, plan = self.p, self.r, self.x, self.back, self.plan
        self.forward()
        self.backward()

        def length(c, pq):
            value = p[c]
            return (pq + value * (back[plan[8, c]] + value),)

        (pq,) = loop(self.slots, 4, length, self.zero)
        a = self.rr / total_of(pq)

        def move(c, nn):
            value = p[c]
            new = r[c] - a * (back[plan[8, c]] + value)
            r[c] = new
            if last:
                x[c] = x[c] + a * value
            return (nn + new * new,)

        (nn,) = loop(self.slots, 4, move, self.zero)
        nn = total_of(nn)
        if last:
            return
        ratio = nn / self.rr

        def turn(c, _):
            value = p[c]
            x[c] = x[c] + a * value
            value = r[c] + ratio * value
            p[c] = value
            split_store(self.p_hl, c, value)
            return (_,)

        loop(self.slots, 4, turn, 0)
        self.rr = nn

    def end(self):
        square = self.forward(square=True)

        def own(c, total):
            return (total + self.p[c] * self.p[c],)

        (pp,) = loop(self.slots, 4, own, square)
        a = self.rr / total_of(pp)

        def move(c, _):
            self.x[c] = self.x[c] + a * self.p[c]
            return (_,)

        loop(self.slots, 4, move, 0)


def fused_kernel(plan, table, tiles_in, observed_in, x_in, u_in, x, u, z_own, gap_out, *scratch):
    (tiles, observed, tiles_hl, r, p, p_hl, image_hl, back, z_before, gap_box, local_sem, gap_send, gap_recv,
     send_sem, recv_sem) = scratch[BOXES * len(ORDERS):]
    boxes = [scratch[n * len(ORDERS):(n + 1) * len(ORDERS)] for n in range(BOXES)]
    loads = [pltpu.make_async_copy(src, dst, local_sem.at[n]) for n, (src, dst) in enumerate(
        ((x_in, x), (u_in, u), (tiles_in, tiles), (observed_in, observed)))]
    for load in loads:
        load.start()
    at = Place()
    barrier = pltpu.get_barrier_semaphore()
    friends = [at.partner]
    for axis in ("x", "y", "z"):
        friends += [at.near(axis, 2)] + [at.near(axis, delta, c) for delta in (1, -1) for c in (0, 1)]
    for friend in friends:
        pl.semaphore_signal(barrier, inc=1, device_id=friend, device_id_type=MESH)
    exchange = Exchange(at, table, SETS[0], 0, boxes, send_sem, recv_sem)
    solver = Solver(plan, tiles_hl, x, u, r, p, p_hl, image_hl, back, z_before)
    loads[0].wait()
    loads[1].wait()
    for part in exchange.parts:
        launch = exchange.start(part, x, u)
        if part == 0:
            pl.semaphore_wait(barrier, len(friends))
        launch()
    loads[2].wait()

    def split_tile(t, _):
        split_store(tiles_hl, t, tiles[t])
        return (_,)

    loop(tiles.shape[0], 2, split_tile, 0)
    back[back.shape[0] - 1] = solver.zero
    loads[3].wait()
    solver.load_x()
    exchange.pass_on()
    solver.forward(observed=observed)
    solver.backward()

    def rest():
        exchange.reduce_first()
        exchange.reduce_second()
        exchange.reduce_third()
        exchange.agree(z_own)
        exchange.spread_first()
        exchange.spread_second()
        exchange.give_back()
        exchange.give_on()
        exchange.finish()

    rest()
    solver.begin(True, exchange.read)
    for number in range(CG_STEPS):
        solver.step(number == CG_STEPS - 1)
    for part in exchange.parts:
        exchange.start(part, x, u)()
    exchange.pass_on()
    rest()
    gap = solver.begin(False, exchange.read)

    gap_moves = []

    def gap_copy(n, device):
        return pltpu.make_async_remote_copy(
            src_ref=gap_box.at[10 + n // 3], dst_ref=gap_box.at[n], send_sem=gap_send.at[n],
            recv_sem=gap_recv.at[n], device_id=device, device_id_type=MESH)

    def gap_stage(stage, value):
        gap_box[10 + stage] = value
        peers = [at.near("xyz"[stage], delta) for delta in (1, 2, 3)] if stage < 3 else [at.partner]
        for n, peer in enumerate(peers):
            moving = gap_copy(3 * stage + n, peer)
            moving.start()
            gap_moves.append(moving)

    def gap_sum(stage):
        value = gap_box[10 + stage]
        for n in range(3 if stage < 3 else 1):
            gap_copy(3 * stage + n, at.partner).wait_recv()
            value = value + gap_box[3 * stage + n]
        return value

    gap_stage(0, gap)
    for number in range(CG_STEPS - 1):
        solver.step(False)
        gap_stage(number + 1, gap_sum(number))
    solver.end()
    gap_out[...] = gap_sum(3)
    for moving in gap_moves:
        moving.wait_send()


def fused(plan, table, tiles, observed, x, u):
    slots, targets, blk = x.shape
    count = tiles.shape[0]
    each = lambda shape: [pltpu.VMEM(shape(t * SUB), F32) for t in SETS[0]]
    scratch = (
        each(lambda r: (8, 16 * r + 16, blk)) + each(lambda r: (8, 16 * r + 16, blk))
        + each(lambda r: (2, 16 * r + 16, blk)) + each(lambda r: (SIDE, SIDE * (PER * r + SUB), blk))
        + each(lambda r: (SIDE * (PER * r + SUB), blk)) + each(lambda r: (2, SIDE * (PER * r + SUB), blk))
        + each(lambda r: (SIDE, PER * r + SUB, blk)) + each(lambda r: (3, PER * r + SUB, blk))
        + each(lambda r: (SIDE, SIDE, PER * r, blk)) + each(lambda r: (128, r, blk))
        + each(lambda r: (128, r, blk)) + each(lambda r: (32, r, blk))
        + [
            pltpu.VMEM(tiles.shape, F32), pltpu.VMEM(observed.shape, F32),
            pltpu.VMEM((count, 2 * blk, blk), BF16), pltpu.VMEM(x.shape, F32), pltpu.VMEM(x.shape, F32),
            pltpu.VMEM((slots, 2 * targets, blk), BF16), pltpu.VMEM((count, 2 * targets, blk), BF16),
            pltpu.VMEM((count + 1, targets, blk), F32), pltpu.VMEM(x.shape, F32),
            pltpu.VMEM((14, targets, blk), F32),
            pltpu.SemaphoreType.DMA((4,)), pltpu.SemaphoreType.DMA((10,)), pltpu.SemaphoreType.DMA((10,)),
            pltpu.SemaphoreType.DMA((len(ORDERS), SEMS)), pltpu.SemaphoreType.DMA((len(ORDERS), SEMS)),
        ]
    )
    whole = pl.BlockSpec(memory_space=pltpu.VMEM)
    scalars = pl.BlockSpec(memory_space=pltpu.SMEM)
    like = jax.ShapeDtypeStruct(x.shape, F32)
    return pl.pallas_call(
        fused_kernel,
        out_shape=(like, like, jax.ShapeDtypeStruct((PER, targets, blk), F32),
                   jax.ShapeDtypeStruct((targets, blk), F32)),
        in_specs=[scalars, scalars] + [pl.BlockSpec(memory_space=pl.ANY)] * 4,
        out_specs=(whole,) * 4,
        scratch_shapes=scratch,
        compiler_params=pltpu.CompilerParams(
            collective_id=0, has_side_effects=True, vmem_limit_bytes=67043328),
        name="consensus",
    )(plan, table, tiles, observed, x, u)


def on_device(tile_data, tile_row, tile_col, tile_count, touched, owner_map, observed, start_x, start_u):
    shards = lax.axis_size(AXES)
    local_cols = touched.shape[1]
    col_blocks = owner_map.shape[0]
    col_dev = col_blocks // shards
    plan = tile_plan(tile_row[0], tile_col[0], tile_count[0])
    wanted = touched[0]
    matches = (wanted[:, None] == jnp.arange(col_blocks, dtype=jnp.int32)[None, :]).astype(jnp.int32)
    position = jnp.sum(matches * owner_map[None, :], axis=1)
    owner = position // col_dev
    table = exchange_plan(owner, position - owner * col_dev, shards)
    flip = lambda a: jnp.swapaxes(a, 1, 2)
    x, u, z, gap = fused(plan, table, tile_data, flip(observed), flip(start_x), flip(start_u))
    primal_gap = jnp.sqrt(jnp.sum(gap, axis=1) / (shards * local_cols * start_x.shape[1]))
    return flip(x), flip(u), flip(z), primal_gap


def solution(mesh):
    split = P(AXES)
    return jax.shard_map(
        on_device, mesh=mesh,
        in_specs=(split, split, split, split, split, P(), split, split, split),
        out_specs=(split, split, split, P()),
        check_vma=False,
    )
```

time: 478 us -> 203 us (0.42)
  waiting for transfers between devices: 171 us -> 0 us
  blocking collectives: 128 us -> 0 us
  Pallas kernels: 70.1 us -> 189 us
  starting transfers between devices: 38.4 us -> 0 us
  local copies, waits for them, and re-layouts: 42.8 us -> 6.58 us
  matrix products: 13.3 us -> 0 us
  other arithmetic: 10.9 us -> 5.95 us
    all_to_all x4 -> x0, waiting for transfers between devices: 171 us -> none  [the longest x2 115 us: consensus(): lax.all_to_all(back, AXES, split_axis=0, concat_axis=0, tiled=True)]
    pallas_call x2 -> x1, Pallas kernels: 70.1 us -> 189 us  [fused(): pl.pallas_call(fused_kernel, out_shape=(like, like, jax.ShapeDtypeStruct(...]
    all_to_all x1 -> x0, blocking collectives: 64.4 us -> none  [consensus(): lax.all_to_all(outbox, AXES, split_axis=0, concat_axis=0, tiled=True)]
    psum x1 -> x0, blocking collectives: 63.4 us -> none  [on_device(): total = lax.psum(jnp.sum(gap, axis=1), AXES)]
    all_to_all x4 -> x0, starting transfers between devices: 38.4 us -> none  [the longest x2 16.6 us: consensus(): lax.all_to_all(back, AXES, split_axis=0, concat_axis=0, tiled=True)]
    scatter x3 -> x0, local copies, waits for them, and re-layouts: 17.9 us -> none  [the longest x2 17.2 us: consensus(): outbox = jnp.zeros((shards,) + block, F32).at[owner].set(merged)]
    dot_general x4 -> x0, matrix products: 13.3 us -> none  [the longest x2 9.57 us: consensus(): jnp.einsum('dy,ysh->dsh', delivery, inbox, precision=lax.Precision.HIGHEST)]
    dot_general x2 -> x0, local copies, waits for them, and re-layouts: 8.8 us -> none  [consensus(): jnp.einsum('pu,pxa->uxa', delivery, z, precision=lax.Precision.HIGHEST)]
  transfers between devices with their start and end apart: 4 -> 0, of which waited for: 3 -> 0; matrix products, arithmetic and copies ran while one was open for 4% -> 0% of each run, Pallas kernels for 0% -> 0%
where the time goes in v3:
time: 203 us
  Pallas kernels  189 us (93%)
  local copies, waits for them, and re-layouts  6.58 us (3%)
  other arithmetic  5.95 us (3%)
    pallas_call x1, Pallas kernels, fused(): pl.pallas_call(fused_kernel, out_shape=(like, like, jax.ShapeDtypeStruct(...  189 us
    unnamed x7, local copies, waits for them, and re-layouts  5.29 us

profile of v3, /device:TPU:1, one launch (start us, length us, event | category | flops | bytes accessed | tf_op | source)
XLA Modules:
  0.0 203.2 jit_solution(8045306496916595547)
XLA Ops:
  1.3 0.9 select_reduce_fusion
  2.2 0.7 iota_add_fusion
  2.9 0.7 add_bitcast_fusion.1
  3.6 0.2 convert_reduce_fusion
  3.8 0.2 convert_reduce_fusion.1
  3.9 0.9 select_reduce_fusion.6
  4.8 0.2 select_reduce_fusion.3
  5.0 0.1 compare_convert_fusion
  5.1 0.1 slice_bitcast_fusion.1
  5.2 0.1 and_convert_fusion
  5.2 1.2 stack.30.plan
  6.5 0.1 select_reduce_fusion.2
  6.6 0.6 pad_add_fusion.table
  7.2 189.3 %consensus.1 = (f32[64,64,128]{2,1,0:T(8,128)}, f32[64,64,128]{2,1,0:T(8,128)}, f32[4,64,128]{2,1,0:T(8,128)}, f32[64,128]{1,0:T(8,128)}) custom-call(s32[9,64]{1,0:T(8,128)} %stack.30.plan, s32[9,128]{1,0:T(8,128)} %pad_add_fusion.table, f32[64,128,128]{2,1,0:T(8,128)} %tiles_in.1, f32[32,64,128]{2,1,0:T(8,128)} %bitcast.105, f32[64,64,128]{2,1,0:T(8,128)} %bitcast.103, ...), custom_call_target="tpu_custom_call" | custom-call | tf_op jit(solution)/shard_map/consensus/pallas_call | solution.py:602
  196.5 0.9 reduce_sum.128
  197.3 0.5 multiply_sqrt_fusion
  197.9 0.0 copy-start
  197.9 3.3 %copy.17 = f32[64,128,64]{1,2,0:T(8,128)} copy(f32[64,128,64]{1,2,0:T(8,128)} %bitcast.102) | data formatting | bytes 4194304
  201.2 0.0 copy-done
  201.2 0.0 copy-start.1
  201.2 1.3 copy.18
  202.5 0.0 copy-done.1
  202.5 0.7 copy.19
  (8 shorter events, 0.1 us)
Async XLA Ops:
  197.9 3.3 %copy-start = (f32[64,64,128]{2,1,0:T(8,128)S(1)}, f32[64,64,128]{2,1,0:T(8,128)}, u32[]{:S(2)}) copy-start(f32[64,64,128]{2,1,0:T(8,128)} %get-tuple-element.9) | copy-start | bytes 6291460
  201.2 1.3 copy-start.1

commit v4 on v3

--- a/solution.py
+++ b/solution.py
@@ -9,7 +9,7 @@
 
 ITERS = 2
 CG_STEPS = 4
-GROUP = 16
+GROUP = 32
 AXES = ("dev", "ka")
 F32 = jnp.float32
 BF16 = jnp.bfloat16
@@ -20,15 +20,16 @@
 PER = 4
 ORDERS = (("x", "y", "z"), ("y", "z", "x"), ("z", "x", "y"))
 SETS = ((3, 3, 2),)
-S1, S1F, S2F, S2S, S2D, S3, T3, T2O, T2F, T2D, T1, T1F, SEMS = 0, 8, 9, 10, 11, 12, 16, 20, 21, 22, 23, 31, 32
-BOXES = 12
+S1, S1F, S2F, S2S, S2D, S3, T3, T2O, T2F, T2D, T1, T1F, SEMS = 0, 8, 9, 13, 17, 21, 25, 29, 33, 37, 41, 49, 50
+THERE, BACK = (2, 1, 3, 0), (0, 1, 3, 2)
+BOXES = 13
 
 
 def fold(values):
     return functools.reduce(lambda s, n: s + n, values)
 
 
-def split_store(ref, index, value):
+def split_tile(ref, index, value):
     rows = value.shape[0]
     high = value.astype(BF16)
     low = (value - high.astype(F32)).astype(BF16)
@@ -36,8 +37,19 @@
     ref[index, rows:, :] = low
 
 
+def split_store(ref, index, value):
+    for n in range(0, value.shape[0], SUB):
+        part = value[n:n + SUB]
+        high = part.astype(BF16).astype(F32)
+        ref[index, 2 * n:2 * n + 2 * SUB, :] = jnp.concatenate([high, part - high], axis=0).astype(BF16)
+
+
 def join(wide, rows, cols):
-    return (wide[:rows, :cols] + wide[:rows, cols:]) + wide[rows:, :cols]
+    pieces = []
+    for n in range(0, 2 * rows, 2 * SUB):
+        high, low = wide[n:n + SUB], wide[n + SUB:n + 2 * SUB]
+        pieces.append((high[:, :cols] + high[:, cols:]) + low[:, :cols])
+    return jnp.concatenate(pieces, axis=0)
 
 
 def total_of(value):
@@ -125,7 +137,8 @@
         self.at, self.table, self.tiles = at, table, tiles
         self.base = [(base + sum(tiles[:p])) * SUB for p in range(len(tiles))]
         (self.mail, self.in1, self.fwd1, self.part2, self.fwd2, self.in2, self.part3, self.in3,
-         self.zb2, self.inbox, self.sel, self.zrel) = boxes
+         self.zb2, self.inbox, self.sel, self.zrel, self.share) = boxes
+        self.first = True
         self.send_sem, self.recv_sem = send_sem, recv_sem
         self.sends = []
         self.parts = range(len(tiles))
@@ -156,12 +169,16 @@
         def record(q, _):
             for i in range(16):
                 slot = table[p, q * 16 + i]
-                tag = table[parts + p, q * 16 + i]
                 mail[q, i * rows:(i + 1) * rows, :] = x[slot, where, :] + u[slot, where, :]
-                mail[q, 16 * rows + i:16 * rows + i + 1, :] = jnp.full((1, x.shape[2]), tag, jnp.int32).astype(F32)
+                if self.first:
+                    tag = table[parts + p, q * 16 + i]
+                    mail[q, 16 * rows + i:16 * rows + i + 1, :] = jnp.full((1, x.shape[2]), tag, jnp.int32).astype(F32)
             return (_,)
 
         loop(8, 1, record, 0)
+
+    def sent_rows(self, p, count, extra):
+        return pl.ds(0, count * self.tiles[p] * SUB + (extra if self.first else 0))
 
     def scatter(self, p, box, into, relay, base, base_f):
         at, a, core = self.at, ORDERS[p][0], self.at.core
@@ -181,16 +198,19 @@
     def start(self, p, x, u):
         self.pack(p, x, u)
 
+        rows = self.sent_rows(p, 16, 16)
+
         def box(place, c):
-            return self.mail[p].at[pl.ds(place * 2, 2)] if c is None else self.mail[p].at[place * 2 + c]
+            return self.mail[p].at[pl.ds(place * 2, 2) if c is None else place * 2 + c, rows]
 
         return lambda: self.scatter(
-            p, box, lambda delta: self.in1[p].at[delta * 2 + self.at.core], self.fwd1[p], S1, S1F)
+            p, box, lambda delta: self.in1[p].at[delta * 2 + self.at.core, rows], self.fwd1[p].at[:, rows], S1, S1F)
 
     def pass_on(self):
         for p in self.parts:
-            fwd = self.fwd1[p]
-            self.relay(p, lambda c: fwd if c is None else fwd.at[c], self.in1[p].at[4 + self.at.core], S1, S1F)
+            fwd, rows = self.fwd1[p], self.sent_rows(p, 16, 16)
+            self.relay(p, lambda c: fwd.at[:, rows] if c is None else fwd.at[c, rows],
+                       self.in1[p].at[4 + self.at.core, rows], S1, S1F)
 
     def sources(self, p):
         at, a = self.at, ORDERS[p][0]
@@ -206,10 +226,9 @@
     def combine(self, p):
         tiles = self.tiles[p]
         rows = tiles * SUB
-        width = PER * rows + SUB
         found = self.sources(p)
         part2 = self.part2[p]
-        blk = part2.shape[2]
+        blk = part2.shape[3]
 
         def some(a2, _):
             for a3 in range(SIDE):
@@ -220,62 +239,76 @@
                     place = pl.multiple_of(i * rows + j * SUB, SUB)
                     data = [read(pl.ds(place, SUB)) for _, _, read in found]
                     for k in range(PER):
-                        start = a3 * width + k * rows + j * SUB
-                        part2[a2, start:start + SUB, :] = fold(
+                        start = k * rows + j * SUB
+                        part2[a2, a3, start:start + SUB, :] = fold(
                             [jnp.where(h, v, 0.0) for h, v in zip(hits[k], data)])
-                for k in range(PER):
-                    start = a3 * width + PER * rows + k
-                    part2[a2, start:start + 1, :] = fold([jnp.where(h, 1.0, 0.0) for h in hits[k]])[:1]
-                start = a3 * width + PER * rows + PER
-                part2[a2, start:start + SUB - PER, :] = jnp.zeros((SUB - PER, blk), F32)
+                if self.first:
+                    counts = [fold([jnp.where(h, 1.0, 0.0) for h in hits[k]])[:1] for k in range(PER)]
+                    counts.append(jnp.zeros((SUB - PER, blk), F32))
+                    part2[a2, a3, PER * rows:PER * rows + SUB, :] = jnp.concatenate(counts, axis=0)
             return (_,)
 
         loop(SIDE, 1, some, 0)
 
     def reduce_first(self):
-        at = self.at
-        for p in self.parts:
-            b = ORDERS[p][1]
-            for delta, c in self.others():
-                self.arrive(p, self.in1[p].at[delta * 2 + c], S1 + delta * 2 + c)
-            self.combine(p)
-            self.go(p, self.part2[p].at[at.ring(b, 2)], self.fwd2[p], S2F, S2F, at.near(b, at.way))
-            self.go(p, self.part2[p].at[at.ring(b, -at.way)], self.in2[p].at[1], S2D, S2D, at.near(b, -at.way))
-
-    def reduce_second(self):
-        at = self.at
-        for p in self.parts:
-            b = ORDERS[p][1]
-            self.arrive(p, self.fwd2[p], S2F)
-            to = at.ring(b, at.way)
-            self.part2[p][to] = self.part2[p][to] + self.fwd2[p][...]
-            self.go(p, self.part2[p].at[to], self.in2[p].at[0], S2S, S2S, at.near(b, at.way))
-
-    def reduce_third(self):
         at = self.at
         for p in self.parts:
             b, d = ORDERS[p][1], ORDERS[p][2]
-            width = PER * self.tiles[p] * SUB + SUB
-            self.arrive(p, self.in2[p].at[1], S2D)
-            self.arrive(p, self.in2[p].at[0], S2S)
-            whole = self.part2[p][at.me[b]] + self.in2[p][0] + self.in2[p][1]
-            for a3 in range(SIDE):
-                self.part3[p][a3] = whole[a3 * width:(a3 + 1) * width]
-            for delta in (2, 1, 3):
-                self.go(p, self.part3[p].at[at.ring(d, delta)], self.in3[p].at[delta - 1],
-                        S3 + delta, S3 + delta, at.near(d, delta))
+            every = self.sent_rows(p, 16, 16)
+            rows = self.sent_rows(p, PER, SUB)
+            for delta, c in self.others():
+                self.arrive(p, self.in1[p].at[delta * 2 + c, every], S1 + delta * 2 + c)
+            self.combine(p)
+            for n, delta in enumerate(THERE):
+                piece = at.ring(d, delta)
+                self.go(p, self.part2[p].at[at.ring(b, 2), piece, rows], self.fwd2[p].at[piece, rows],
+                        S2F + n, S2F + n, at.near(b, at.way))
+            for n, delta in enumerate(THERE):
+                piece = at.ring(d, delta)
+                self.go(p, self.part2[p].at[at.ring(b, -at.way), piece, rows], self.in2[p].at[1, piece, rows],
+                        S2D + n, S2D + n, at.near(b, -at.way))
+
+    def reduce_second(self):
+        at = self.at
+        for n, delta in enumerate(THERE):
+            for p in self.parts:
+                b, piece = ORDERS[p][1], at.ring(ORDERS[p][2], delta)
+                rows = self.sent_rows(p, PER, SUB)
+                self.arrive(p, self.fwd2[p].at[piece, rows], S2F + n)
+                to = at.ring(b, at.way)
+                self.part2[p][to, piece, rows, :] = self.part2[p][to, piece, rows, :] + self.fwd2[p][piece, rows, :]
+                self.go(p, self.part2[p].at[to, piece, rows], self.in2[p].at[0, piece, rows],
+                        S2S + n, S2S + n, at.near(b, at.way))
+
+    def reduce_third(self):
+        at = self.at
+        for n, delta in enumerate(THERE):
+            for p in self.parts:
+                b, d = ORDERS[p][1], ORDERS[p][2]
+                piece = at.ring(d, delta)
+                rows = self.sent_rows(p, PER, SUB)
+                self.arrive(p, self.in2[p].at[1, piece, rows], S2D + n)
+                self.arrive(p, self.in2[p].at[0, piece, rows], S2S + n)
+                self.part3[p][piece, rows, :] = (
+                    self.part2[p][at.me[b], piece, rows, :] + self.in2[p][0, piece, rows, :]
+                    + self.in2[p][1, piece, rows, :])
+                if delta:
+                    self.go(p, self.part3[p].at[piece, rows], self.in3[p].at[delta - 1, rows],
+                            S3 + delta, S3 + delta, at.near(d, delta))
 
     def agree(self, z_own):
         at = self.at
         for p in self.parts:
             b, d = ORDERS[p][1], ORDERS[p][2]
             rows, base = self.tiles[p] * SUB, self.base[p]
+            every = self.sent_rows(p, PER, SUB)
             for delta in (1, 3, 2):
-                self.arrive(p, self.in3[p].at[delta - 1], S3 + delta)
-            whole = ((self.part3[p][at.me[d]] + self.in3[p][0]) + self.in3[p][1]) + self.in3[p][2]
+                self.arrive(p, self.in3[p].at[delta - 1, every], S3 + delta)
+            whole = fold([self.part3[p][at.me[d], every, :]] + [self.in3[p][n, every, :] for n in range(3)])
+            if self.first:
+                self.share[p][...] = jnp.maximum(whole[PER * rows:], 1.0)
             for k in range(PER):
-                number = whole[PER * rows + k:PER * rows + k + 1]
-                share = jnp.maximum(number, 1.0)
+                share = self.share[p][k:k + 1, :]
                 value = whole[k * rows:(k + 1) * rows] / share
                 cut = jnp.broadcast_to(1.0 / share, value.shape)
                 value = value - jnp.minimum(jnp.maximum(value, -cut), cut)
@@ -284,24 +317,27 @@
             own = self.zb2[p].at[at.me[b], at.me[d]]
             for delta in (2, 1, 3):
                 self.go(p, own, own, T3 + delta, T3 + delta, at.near(d, delta))
-
-    def spread_first(self):
-        at = self.at
-        for p in self.parts:
-            b, d = ORDERS[p][1], ORDERS[p][2]
-            for delta in (1, 3, 2):
-                self.arrive(p, self.zb2[p].at[at.me[b], at.ring(d, -delta)], T3 + delta)
-            own = self.zb2[p].at[at.me[b]]
-            self.go(p, own, own, T2O, T2O, at.near(b, at.way))
-            self.go(p, own, own, T2D, T2D, at.near(b, -at.way))
-
-    def spread_second(self):
-        at = self.at
-        for p in self.parts:
-            b = ORDERS[p][1]
-            passing = self.zb2[p].at[at.ring(b, -at.way)]
-            self.arrive(p, passing, T2O)
-            self.go(p, passing, passing, T2F, T2F, at.near(b, at.way))
+            self.spread(p, 0)
+
+    def spread(self, p, n):
+        at, b = self.at, ORDERS[p][1]
+        own = self.zb2[p].at[at.me[b], at.ring(ORDERS[p][2], -BACK[n])]
+        if n:
+            self.arrive(p, own, T3 + BACK[n])
+        self.go(p, own, own, T2O + n, T2O + n, at.near(b, at.way))
+        self.go(p, own, own, T2D + n, T2D + n, at.near(b, -at.way))
+
+    def spread_on(self, p, n):
+        at, b = self.at, ORDERS[p][1]
+        passing = self.zb2[p].at[at.ring(b, -at.way), at.ring(ORDERS[p][2], -BACK[n])]
+        self.arrive(p, passing, T2O + n)
+        self.go(p, passing, passing, T2F + n, T2F + n, at.near(b, at.way))
+
+    def spread_all(self):
+        for act, n in ((self.spread, 1), (self.spread, 2), (self.spread_on, 0), (self.spread, 3),
+                       (self.spread_on, 1), (self.spread_on, 2), (self.spread_on, 3)):
+            for p in self.parts:
+                act(p, n)
 
     def select(self, p):
         at = self.at
@@ -333,8 +369,10 @@
         self.sent()
         for p in self.parts:
             a, b = ORDERS[p][0], ORDERS[p][1]
-            self.arrive(p, self.zb2[p].at[at.ring(b, at.way)], T2D)
-            self.arrive(p, self.zb2[p].at[at.ring(b, 2)], T2F)
+            for n, delta in enumerate(BACK):
+                piece = at.ring(ORDERS[p][2], -delta)
+                self.arrive(p, self.zb2[p].at[at.ring(b, at.way), piece], T2D + n)
+                self.arrive(p, self.zb2[p].at[at.ring(b, 2), piece], T2F + n)
             self.select(p)
             sel = self.sel[p]
 
@@ -373,7 +411,7 @@
         self.targets = p_hl.shape[1] // 2
         self.zero = jnp.zeros((self.targets, self.blk), F32)
 
-    def forward(self, observed=None, square=False):
+    def forward(self, observed=None):
         plan, targets, blk = self.plan, self.targets, self.blk
 
         def tile_step(k, acc, total):
@@ -381,12 +419,11 @@
                 self.p_hl[plan[1, k]], self.tiles_hl[plan[0, k]], (((1,), (1,)), ((), ())),
                 preferred_element_type=F32)
             acc = jnp.where(plan[2, k] > 0, acc, 0.0) + join(wide, targets, blk)
-            if square:
-                total = total + jnp.where(plan[3, k] > 0, acc * acc, 0.0)
-            elif observed is not None:
+            if observed is not None:
                 split_store(self.image_hl, k, observed[plan[4, k]] - acc)
             else:
                 split_store(self.image_hl, k, acc)
+                total = total + jnp.where(plan[3, k] > 0, acc * acc, 0.0)
             return acc, total
 
         return loop(self.slots, GROUP, tile_step, self.zero, self.zero)[1]
@@ -428,60 +465,50 @@
             return rr + r * r, gap + diff * diff
 
         rr, gap = loop(self.slots, 4, one, self.zero, self.zero)
+        self.own = rr
         self.rr = total_of(rr)
         return gap
 
-    def step(self, last):
-        p, r, x, back, plan = self.p, self.r, self.x, self.back, self.plan
-        self.forward()
+    def length(self):
+        self.a = self.rr / total_of(self.forward() + self.own)
+
+    def move_x(self):
+        p, x, a = self.p, self.x, self.a
+
+        def move(c, _):
+            x[c] = x[c] + a * p[c]
+            return (_,)
+
+        loop(self.slots, 4, move, 0)
+
+    def move_r(self):
+        p, r, back, plan, a = self.p, self.r, self.back, self.plan, self.a
         self.backward()
 
-        def length(c, pq):
-            value = p[c]
-            return (pq + value * (back[plan[8, c]] + value),)
-
-        (pq,) = loop(self.slots, 4, length, self.zero)
-        a = self.rr / total_of(pq)
-
         def move(c, nn):
-            value = p[c]
-            new = r[c] - a * (back[plan[8, c]] + value)
+            new = r[c] - a * (back[plan[8, c]] + p[c])
             r[c] = new
-            if last:
-                x[c] = x[c] + a * value
             return (nn + new * new,)
 
-        (nn,) = loop(self.slots, 4, move, self.zero)
-        nn = total_of(nn)
-        if last:
-            return
+        return loop(self.slots, 4, move, self.zero)[0]
+
+    def step(self):
+        p, r, x = self.p, self.r, self.x
+        self.length()
+        a = self.a
+        nn = total_of(self.move_r())
         ratio = nn / self.rr
 
-        def turn(c, _):
+        def turn(c, own):
             value = p[c]
             x[c] = x[c] + a * value
             value = r[c] + ratio * value
             p[c] = value
             split_store(self.p_hl, c, value)
-            return (_,)
-
-        loop(self.slots, 4, turn, 0)
+            return (own + value * value,)
+
+        self.own = loop(self.slots, 4, turn, self.zero)[0]
         self.rr = nn
-
-    def end(self):
-        square = self.forward(square=True)
-
-        def own(c, total):
-            return (total + self.p[c] * self.p[c],)
-
-        (pp,) = loop(self.slots, 4, own, square)
-        a = self.rr / total_of(pp)
-
-        def move(c, _):
-            self.x[c] = self.x[c] + a * self.p[c]
-            return (_,)
-
-        loop(self.slots, 4, move, 0)
 
 
 def fused_kernel(plan, table, tiles_in, observed_in, x_in, u_in, x, u, z_own, gap_out, *scratch):
@@ -510,11 +537,11 @@
         launch()
     loads[2].wait()
 
-    def split_tile(t, _):
-        split_store(tiles_hl, t, tiles[t])
+    def one_tile(t, _):
+        split_tile(tiles_hl, t, tiles[t])
         return (_,)
 
-    loop(tiles.shape[0], 2, split_tile, 0)
+    loop(tiles.shape[0], 2, one_tile, 0)
     back[back.shape[0] - 1] = solver.zero
     loads[3].wait()
     solver.load_x()
@@ -527,18 +554,21 @@
         exchange.reduce_second()
         exchange.reduce_third()
         exchange.agree(z_own)
-        exchange.spread_first()
-        exchange.spread_second()
+        exchange.spread_all()
         exchange.give_back()
         exchange.give_on()
         exchange.finish()
 
     rest()
     solver.begin(True, exchange.read)
-    for number in range(CG_STEPS):
-        solver.step(number == CG_STEPS - 1)
+    for number in range(CG_STEPS - 1):
+        solver.step()
+    solver.length()
+    solver.move_x()
+    exchange.first = False
     for part in exchange.parts:
         exchange.start(part, x, u)()
+    solver.move_r()
     exchange.pass_on()
     rest()
     gap = solver.begin(False, exchange.read)
@@ -567,9 +597,10 @@
 
     gap_stage(0, gap)
     for number in range(CG_STEPS - 1):
-        solver.step(False)
+        solver.step()
         gap_stage(number + 1, gap_sum(number))
-    solver.end()
+    solver.length()
+    solver.move_x()
     gap_out[...] = gap_sum(3)
     for moving in gap_moves:
         moving.wait_send()
@@ -581,11 +612,11 @@
     each = lambda shape: [pltpu.VMEM(shape(t * SUB), F32) for t in SETS[0]]
     scratch = (
         each(lambda r: (8, 16 * r + 16, blk)) + each(lambda r: (8, 16 * r + 16, blk))
-        + each(lambda r: (2, 16 * r + 16, blk)) + each(lambda r: (SIDE, SIDE * (PER * r + SUB), blk))
-        + each(lambda r: (SIDE * (PER * r + SUB), blk)) + each(lambda r: (2, SIDE * (PER * r + SUB), blk))
+        + each(lambda r: (2, 16 * r + 16, blk)) + each(lambda r: (SIDE, SIDE, PER * r + SUB, blk))
+        + each(lambda r: (SIDE, PER * r + SUB, blk)) + each(lambda r: (2, SIDE, PER * r + SUB, blk))
         + each(lambda r: (SIDE, PER * r + SUB, blk)) + each(lambda r: (3, PER * r + SUB, blk))
         + each(lambda r: (SIDE, SIDE, PER * r, blk)) + each(lambda r: (128, r, blk))
-        + each(lambda r: (128, r, blk)) + each(lambda r: (32, r, blk))
+        + each(lambda r: (128, r, blk)) + each(lambda r: (32, r, blk)) + each(lambda r: (SUB, blk))
         + [
             pltpu.VMEM(tiles.shape, F32), pltpu.VMEM(observed.shape, F32),
             pltpu.VMEM((count, 2 * blk, blk), BF16), pltpu.VMEM(x.shape, F32), pltpu.VMEM(x.shape, F32),

time: 203 us -> 187 us (0.921)
  Pallas kernels: 189 us -> 173 us
    pallas_call x1, Pallas kernels: 189 us -> 173 us  [fused(): pl.pallas_call(fused_kernel, out_shape=(like, like, jax.ShapeDtypeStruct(...]
where the time goes in v4:
time: 187 us
  Pallas kernels  173 us (93%)
  local copies, waits for them, and re-layouts  6.58 us (4%)
  other arithmetic  5.95 us (3%)
    pallas_call x1, Pallas kernels, fused(): pl.pallas_call(fused_kernel, out_shape=(like, like, jax.ShapeDtypeStruct(...  173 us
    unnamed x7, local copies, waits for them, and re-layouts  5.29 us

profile of v4, /device:TPU:1, one launch (start us, length us, event | category | flops | bytes accessed | tf_op | source)
XLA Modules:
  0.0 186.5 jit_solution(9378283258126857439)
XLA Ops:
  1.3 0.9 select_reduce_fusion
  2.2 0.7 iota_add_fusion
  2.9 0.7 add_bitcast_fusion.1
  3.6 0.2 convert_reduce_fusion
  3.8 0.2 convert_reduce_fusion.1
  3.9 0.9 select_reduce_fusion.6
  4.8 0.2 select_reduce_fusion.3
  5.0 0.1 compare_convert_fusion
  5.1 0.1 slice_bitcast_fusion.1
  5.2 0.1 and_convert_fusion
  5.2 1.2 stack.30.plan
  6.5 0.1 select_reduce_fusion.2
  6.6 0.6 pad_add_fusion.table
  7.2 172.6 %consensus.1 = (f32[64,64,128]{2,1,0:T(8,128)}, f32[64,64,128]{2,1,0:T(8,128)}, f32[4,64,128]{2,1,0:T(8,128)}, f32[64,128]{1,0:T(8,128)}) custom-call(s32[9,64]{1,0:T(8,128)} %stack.30.plan, s32[9,128]{1,0:T(8,128)} %pad_add_fusion.table, f32[64,128,128]{2,1,0:T(8,128)} %tiles_in.1, f32[32,64,128]{2,1,0:T(8,128)} %bitcast.105, f32[64,64,128]{2,1,0:T(8,128)} %bitcast.103, ...), custom_call_target="tpu_custom_call" | custom-call | tf_op jit(solution)/shard_map/consensus/pallas_call | solution.py:633
  179.8 0.9 reduce_sum.128
  180.7 0.5 multiply_sqrt_fusion
  181.2 0.0 copy-start
  181.2 3.3 %copy.17 = f32[64,128,64]{1,2,0:T(8,128)} copy(f32[64,128,64]{1,2,0:T(8,128)} %bitcast.102) | data formatting | bytes 4194304
  184.5 0.0 copy-done
  184.5 0.0 copy-start.1
  184.5 1.3 copy.18
  185.9 0.0 copy-done.1
  185.9 0.7 copy.19
  (8 shorter events, 0.1 us)
Async XLA Ops:
  181.2 3.3 %copy-start = (f32[64,64,128]{2,1,0:T(8,128)S(1)}, f32[64,64,128]{2,1,0:T(8,128)}, u32[]{:S(2)}) copy-start(f32[64,64,128]{2,1,0:T(8,128)} %get-tuple-element.9) | copy-start | bytes 6291460
  184.5 1.3 copy-start.1

commit v5 on v4

v5 whole, which is shorter than its diff:
```python
import functools

import jax
import jax.numpy as jnp
from jax import lax
from jax.experimental import pallas as pl
from jax.experimental.pallas import tpu as pltpu
from jax.sharding import PartitionSpec as P

ITERS = 2
CG_STEPS = 4
GROUP = 32
AXES = ("dev", "ka")
F32 = jnp.float32
BF16 = jnp.bfloat16
MESH = pl.DeviceIdType.MESH

SIDE = 4
SUB = 8
PER = 4
ORDERS = (("x", "y", "z"), ("y", "z", "x"), ("z", "x", "y"))
ROWS = (22, 22, 20)
DEEP = 24
S1, S1F, S2F, S2S, S2D, S3, T3, T2O, T2F, T2D, T1, T1F, SEMS = 0, 8, 9, 13, 17, 21, 25, 29, 33, 37, 41, 49, 50
THERE, BACK = (2, 1, 3, 0), (0, 1, 3, 2)
BOXES = 13


def fold(values):
    return functools.reduce(lambda s, n: s + n, values)


def split_tile(ref, index, value):
    rows = value.shape[0]
    high = value.astype(BF16)
    low = (value - high.astype(F32)).astype(BF16)
    ref[index, :rows, :] = high
    ref[index, rows:, :] = low


def split_store(ref, index, value):
    for n in range(0, value.shape[0], SUB):
        part = value[n:n + SUB]
        high = part.astype(BF16).astype(F32)
        ref[index, 2 * n:2 * n + 2 * SUB, :] = jnp.concatenate([high, part - high], axis=0).astype(BF16)


def join(wide, rows, cols):
    pieces = []
    for n in range(0, 2 * rows, 2 * SUB):
        high, low = wide[n:n + SUB], wide[n + SUB:n + 2 * SUB]
        pieces.append((high[:, :cols] + high[:, cols:]) + low[:, :cols])
    return jnp.concatenate(pieces, axis=0)


def total_of(value):
    return jnp.sum(value, axis=1, keepdims=True)


def tables_kernel(rows, cols, touched, owner_map, count, out):
    tiles, lanes = rows.shape[1], out.shape[1]
    near, far = (lax.broadcasted_iota(jnp.int32, (tiles, lanes), n) for n in (0, 1))
    down = lax.broadcasted_iota(jnp.int32, (tiles, 1), 0).astype(F32)
    across = lax.broadcasted_iota(jnp.int32, (1, lanes), 1).astype(F32)
    eye = near == far
    wide = lambda v: jnp.concatenate([v[...].astype(F32), jnp.zeros((1, lanes - tiles), F32)], axis=1)
    stand = lambda v: jnp.sum(jnp.where(eye, v, 0.0), axis=1, keepdims=True)
    lie = lambda v: jnp.sum(jnp.where(eye, v, 0.0), axis=0, keepdims=True)
    ones = lambda m: jnp.where(m, 1.0, 0.0)
    left = lambda m: jnp.sum(ones(m), axis=1, keepdims=True)
    up = lambda m: jnp.sum(ones(m), axis=0, keepdims=True)
    number = count[0].astype(F32)
    inside = across < float(tiles)

    def order(values):
        key = jnp.where(across < number, wide(values), float(tiles))
        key = jnp.where(inside, key, float(tiles + 1))
        code = key * float(lanes) + across
        key_d, code_d = stand(key), stand(code)
        same = key == key_d
        rank = left(code < code_d)
        last = left(key <= key_d) - 1.0
        keep = left(same & (code < code_d))
        later = left(same & (code > code_d))
        ends = jnp.where((later == 0.0) & (key_d < float(tiles)), 1.0, 0.0)
        return key_d, rank, last, keep, ends

    def sort(rank, values):
        return jnp.sum(jnp.where(rank == across, values, 0.0), axis=0, keepdims=True)

    row_d, rank_f, last_f, keep_f, ends_f = order(rows)
    col_d, rank_b, _, keep_b, _ = order(cols)
    found = up(col_d == across)
    until = up(col_d <= across) - 1.0
    last_b = jnp.where(found > 0.0, until, float(tiles))
    plan = [
        sort(rank_f, down), sort(rank_f, stand(wide(cols))), sort(rank_f, keep_f), sort(rank_f, ends_f),
        sort(rank_f, stand(wide(rows))), sort(rank_b, down), sort(rank_b, last_f), sort(rank_b, keep_b), last_b,
    ]
    wanted = stand(wide(touched))
    blocks = owner_map.shape[1]
    every = lax.broadcasted_iota(jnp.int32, (1, blocks), 1).astype(F32)
    position = jnp.sum(jnp.where(wanted == every, owner_map[...].astype(F32), 0.0), axis=1, keepdims=True)
    position = position.astype(jnp.int32)
    owner, tag = position >> 2, (position & 3).astype(F32)
    place = {"x": (owner >> 3) & 3, "y": owner >> 5, "z": owner & 3}
    core = (owner >> 2) & 1
    slots, marks, index = [], [], []
    for a, b, c in ORDERS:
        at = (place[a] * 32 + core * 16 + place[b] * 4 + place[c]).astype(F32)
        match = at == across
        slots.append(jnp.sum(jnp.where(match, down, 0.0), axis=0, keepdims=True))
        marks.append(jnp.sum(jnp.where(match, tag + 1.0, 0.0), axis=0, keepdims=True) - 1.0)
        index.append(lie(at))
    found = slots + marks + index + plan
    for n, row in enumerate(found):
        out[n:n + 1, :] = row.astype(jnp.int32)
    out[len(found):, :] = jnp.zeros((out.shape[0] - len(found), lanes), jnp.int32)


def tables(rows, cols, touched, owner_map, count):
    whole = pl.BlockSpec(memory_space=pltpu.VMEM)
    return pl.pallas_call(
        tables_kernel,
        out_shape=jax.ShapeDtypeStruct((24, 128), jnp.int32),
        in_specs=[whole] * 4 + [pl.BlockSpec(memory_space=pltpu.SMEM)],
        out_specs=whole,
        name="tables",
    )(rows, cols, touched, owner_map.reshape(1, -1), count)


def loop(count, step, body, *init):
    def group(g, carry):
        for n in range(step):
            carry = body(g * step + n, *carry)
        return carry

    return lax.fori_loop(0, count // step, group, init)


def near_device(me, axis, delta, to_core):
    at = dict(me)
    at[axis] = lax.rem(me[axis] + delta + SIDE, SIDE)
    return ((at["y"] * SIDE + at["x"]) * 2 + to_core, at["z"])


class Place:
    def __init__(self):
        dev, z = lax.axis_index("dev"), lax.axis_index("ka")
        self.core = lax.rem(dev, 2)
        self.me = {"x": lax.rem(dev // 2, SIDE), "y": dev // 8, "z": z}
        self.way = 1 - 2 * self.core
        self.partner = (dev + 1 - 2 * self.core, z)

    def near(self, axis, delta, to_core=None):
        return near_device(self.me, axis, delta, self.core if to_core is None else to_core)

    def ring(self, axis, delta):
        return lax.rem(self.me[axis] + delta + SIDE, SIDE)


def row_number(blk):
    return lax.broadcasted_iota(jnp.int32, (SUB, blk), 0)


def part_of(p, ref, slot):
    tile = lambda n: ref[slot, n * SUB:(n + 1) * SUB, :]
    pair = [tile(2 * p), tile(2 * p + 1)]
    if p == 0:
        return pair + [tile(6)]
    if p == 1:
        return pair + [pltpu.roll(tile(7), 6, 0)]
    edge = row_number(ref.shape[2]) < 2
    return pair + [jnp.where(edge, pltpu.roll(tile(6), 2, 0), pltpu.roll(tile(7), 2, 0))]


def from_parts(found):
    row = row_number(found[0].shape[1])
    shared = pltpu.roll(found[2][2 * SUB:], 6, 0)
    six = jnp.where(row < 6, found[0][2 * SUB:], shared)
    seven = jnp.where(row < 2, shared, pltpu.roll(found[1][2 * SUB:], 2, 0))
    return jnp.concatenate([f[:2 * SUB] for f in found] + [six, seven], axis=0)


class Exchange:
    def __init__(self, at, table, boxes, send_sem, recv_sem):
        self.at, self.table = at, table
        (self.mail, self.in1, self.fwd1, self.part2, self.fwd2, self.in2, self.part3, self.in3,
         self.zb2, self.inbox, self.sel, self.zrel, self.share) = boxes
        self.first = True
        self.send_sem, self.recv_sem = send_sem, recv_sem
        self.sends = []
        self.parts = range(len(ORDERS))

    def copy(self, p, src, dst, send, recv, device):
        return pltpu.make_async_remote_copy(
            src_ref=src, dst_ref=dst, send_sem=self.send_sem.at[p, send], recv_sem=self.recv_sem.at[p, recv],
            device_id=device, device_id_type=MESH)

    def go(self, p, src, dst, send, recv, device):
        moving = self.copy(p, src, dst, send, recv, device)
        moving.start()
        self.sends.append(moving)

    def arrive(self, p, dst, recv):
        self.copy(p, dst, dst, 0, recv, self.at.partner).wait_recv()

    def sent(self):
        for moving in self.sends:
            moving.wait_send()
        self.sends = []

    def pack(self, p, x, u):
        table, parts, mail = self.table, len(ORDERS), self.mail[p]

        def record(q, _):
            for i in range(16):
                slot = table[p, q * 16 + i]
                for n, (one, two) in enumerate(zip(part_of(p, x, slot), part_of(p, u, slot))):
                    mail[q, i, n * SUB:(n + 1) * SUB, :] = one + two
                tag = table[parts + p, q * 16 + i]
                mail[q, i, ROWS[p]:ROWS[p] + 1, :] = jnp.full((1, x.shape[2]), tag, jnp.int32).astype(F32)
            return (_,)

        loop(8, 1, record, 0)

    def marked(self, p):
        return pl.ds(0, ROWS[p] + (1 if self.first else 0))

    def scatter(self, p, box, into, relay, base, base_f):
        at, a, core = self.at, ORDERS[p][0], self.at.core
        self.go(p, box(at.ring(a, 2), None), relay, base_f, base_f, at.near(a, at.way))
        for delta in (1, 3):
            for c in (0, 1):
                self.go(p, box(at.ring(a, delta), c), into(delta), base + delta * 2 + c,
                        base + delta * 2 + core, at.near(a, delta, c))
        self.go(p, box(at.me[a], 1 - core), into(0), base, base + core, at.partner)

    def relay(self, p, relay, into, base, base_f):
        at, a = self.at, ORDERS[p][0]
        self.arrive(p, relay(None), base_f)
        for c in (0, 1):
            self.go(p, relay(c), into, base + 4 + c, base + 4 + at.core, at.near(a, at.way, c))

    def start(self, p, x, u):
        self.pack(p, x, u)

        rows = self.marked(p)

        def box(place, c):
            return self.mail[p].at[pl.ds(place * 2, 2) if c is None else place * 2 + c, :, rows]

        return lambda: self.scatter(
            p, box, lambda delta: self.in1[p].at[delta * 2 + self.at.core, :, rows], self.fwd1[p].at[:, :, rows],
            S1, S1F)

    def pass_on(self):
        for p in self.parts:
            fwd, rows = self.fwd1[p], self.marked(p)
            self.relay(p, lambda c: fwd.at[:, :, rows] if c is None else fwd.at[c, :, rows],
                       self.in1[p].at[4 + self.at.core, :, rows], S1, S1F)

    def sources(self, p):
        at, a = self.at, ORDERS[p][0]
        mail, in1 = self.mail[p], self.in1[p]
        found = [(0, at.core, lambda i, rows: mail[at.me[a] * 2 + at.core, i, rows, :])]
        for delta, c in ((0, 1 - at.core), (1, 0), (1, 1), (2, 0), (2, 1), (3, 0), (3, 1)):
            found.append((delta, c, lambda i, rows, n=delta * 2 + c: in1[n, i, rows, :]))
        return found

    def others(self):
        return ((1, 0), (1, 1), (3, 0), (3, 1), (0, 1 - self.at.core), (2, 0), (2, 1))

    def combine(self, p):
        found = self.sources(p)
        part2 = self.part2[p]
        blk = part2.shape[4]
        mark = ROWS[p] - 2 * SUB

        def some(a2, _):
            for a3 in range(SIDE):
                i = a2 * SIDE + a3
                tags = [jnp.broadcast_to(read(i, pl.ds(ROWS[p], 1)), (SUB, blk)) for _, _, read in found]
                hits = [[tag == float(k) for tag in tags] for k in range(PER)]
                for j in range(DEEP // SUB):
                    data = [read(i, pl.ds(j * SUB, SUB)) for _, _, read in found]
                    for k in range(PER):
                        value = fold([jnp.where(h, v, 0.0) for h, v in zip(hits[k], data)])
                        if self.first and j == 2:
                            count = fold([jnp.where(h, 1.0, 0.0) for h in hits[k]])
                            value = jnp.where(row_number(blk) == mark, count, value)
                        part2[a2, a3, k, j * SUB:(j + 1) * SUB, :] = value
            return (_,)

        loop(SIDE, 1, some, 0)

    def reduce_first(self):
        at = self.at
        for p in self.parts:
            b, d = ORDERS[p][1], ORDERS[p][2]
            rows = self.marked(p)
            for delta, c in self.others():
                self.arrive(p, self.in1[p].at[delta * 2 + c, :, rows], S1 + delta * 2 + c)
            self.combine(p)
            for n, delta in enumerate(THERE):
                piece = at.ring(d, delta)
                self.go(p, self.part2[p].at[at.ring(b, 2), piece, :, rows], self.fwd2[p].at[piece, :, rows],
                        S2F + n, S2F + n, at.near(b, at.way))
            for n, delta in enumerate(THERE):
                piece = at.ring(d, delta)
                self.go(p, self.part2[p].at[at.ring(b, -at.way), piece, :, rows], self.in2[p].at[1, piece, :, rows],
                        S2D + n, S2D + n, at.near(b, -at.way))

    def reduce_second(self):
        at = self.at
        for n, delta in enumerate(THERE):
            for p in self.parts:
                b, piece = ORDERS[p][1], at.ring(ORDERS[p][2], delta)
                rows = self.marked(p)
                self.arrive(p, self.fwd2[p].at[piece, :, rows], S2F + n)
                to = at.ring(b, at.way)
                self.part2[p][to, piece] = self.part2[p][to, piece] + self.fwd2[p][piece]
                self.go(p, self.part2[p].at[to, piece, :, rows], self.in2[p].at[0, piece, :, rows],
                        S2S + n, S2S + n, at.near(b, at.way))

    def reduce_third(self):
        at = self.at
        for n, delta in enumerate(THERE):
            for p in self.parts:
                b, d = ORDERS[p][1], ORDERS[p][2]
                piece = at.ring(d, delta)
                rows = self.marked(p)
                self.arrive(p, self.in2[p].at[1, piece, :, rows], S2D + n)
                self.arrive(p, self.in2[p].at[0, piece, :, rows], S2S + n)
                self.part3[p][piece] = (
                    self.part2[p][at.me[b], piece] + self.in2[p][0, piece] + self.in2[p][1, piece])
                if delta:
                    self.go(p, self.part3[p].at[piece, :, rows], self.in3[p].at[delta - 1, :, rows],
                            S3 + delta, S3 + delta, at.near(d, delta))

    def agree(self):
        at = self.at
        for p in self.parts:
            b, d = ORDERS[p][1], ORDERS[p][2]
            rows = self.marked(p)
            for delta in (1, 3, 2):
                self.arrive(p, self.in3[p].at[delta - 1, :, rows], S3 + delta)
            for k in range(PER):
                value = fold([self.part3[p][at.me[d], k]] + [self.in3[p][n, k] for n in range(3)])
                if self.first:
                    self.share[p][k:k + 1, :] = jnp.maximum(value[ROWS[p]:ROWS[p] + 1], 1.0)
                share = self.share[p][k:k + 1, :]
                value = value / share
                cut = jnp.broadcast_to(1.0 / share, value.shape)
                self.zb2[p][at.me[b], at.me[d], k] = value - jnp.minimum(jnp.maximum(value, -cut), cut)
            own = self.zb2[p].at[at.me[b], at.me[d], :, pl.ds(0, ROWS[p])]
            for delta in (2, 1, 3):
                self.go(p, own, own, T3 + delta, T3 + delta, at.near(d, delta))
            self.spread(p, 0)

    def keep(self, z_own):
        at = self.at
        for k in range(PER):
            z_own[k] = from_parts([self.zb2[p][at.me[ORDERS[p][1]], at.me[ORDERS[p][2]], k] for p in self.parts])

    def spread(self, p, n):
        at, b = self.at, ORDERS[p][1]
        own = self.zb2[p].at[at.me[b], at.ring(ORDERS[p][2], -BACK[n]), :, pl.ds(0, ROWS[p])]
        if n:
            self.arrive(p, own, T3 + BACK[n])
        self.go(p, own, own, T2O + n, T2O + n, at.near(b, at.way))
        self.go(p, own, own, T2D + n, T2D + n, at.near(b, -at.way))

    def spread_on(self, p, n):
        at, b = self.at, ORDERS[p][1]
        passing = self.zb2[p].at[at.ring(b, -at.way), at.ring(ORDERS[p][2], -BACK[n]), :, pl.ds(0, ROWS[p])]
        self.arrive(p, passing, T2O + n)
        self.go(p, passing, passing, T2F + n, T2F + n, at.near(b, at.way))

    def spread_all(self):
        for act, n in ((self.spread, 1), (self.spread, 2), (self.spread_on, 0), (self.spread, 3),
                       (self.spread_on, 1), (self.spread_on, 2), (self.spread_on, 3)):
            for p in self.parts:
                act(p, n)

    def select(self, p):
        at = self.at
        a = ORDERS[p][0]
        found = self.sources(p)
        zb2, inbox, sel = self.zb2[p], self.inbox[p], self.sel[p]
        tiles = [slice(j * SUB, (j + 1) * SUB) for j in range(DEEP // SUB)]

        def some(a2, _):
            for a3 in range(SIDE):
                i = a2 * SIDE + a3
                blocks = [[zb2[a2, a3, k, rows, :] for rows in tiles] for k in range(PER)]
                for number, (delta, c, read) in enumerate(found):
                    tag = jnp.broadcast_to(read(i, pl.ds(ROWS[p], 1)), blocks[0][0].shape)
                    hit = [tag == float(k) for k in range(PER - 1)]
                    for j, rows in enumerate(tiles):
                        value = blocks[PER - 1][j]
                        for k in range(PER - 1):
                            value = jnp.where(hit[k], blocks[k][j], value)
                        place = (at.ring(a, -delta) * 2 + c) * 16 + i
                        (sel if number else inbox)[place, rows, :] = value
            return (_,)

        loop(SIDE, 1, some, 0)

    def give_back(self):
        at = self.at
        self.sent()
        for p in self.parts:
            a, b = ORDERS[p][0], ORDERS[p][1]
            rows = pl.ds(0, ROWS[p])
            for n, delta in enumerate(BACK):
                piece = at.ring(ORDERS[p][2], -delta)
                self.arrive(p, self.zb2[p].at[at.ring(b, at.way), piece, :, rows], T2D + n)
                self.arrive(p, self.zb2[p].at[at.ring(b, 2), piece, :, rows], T2F + n)
            self.select(p)
            sel = self.sel[p]

            def box(place, c):
                return sel.at[pl.ds(place * 32, 32) if c is None else pl.ds((place * 2 + c) * 16, 16), rows]

            mine = self.inbox[p].at[pl.ds((at.me[a] * 2 + at.core) * 16, 16), rows]
            self.scatter(p, box, lambda delta: mine, self.zrel[p].at[:, rows], T1, T1F)

    def give_on(self):
        at = self.at
        for p in self.parts:
            zrel, a = self.zrel[p], ORDERS[p][0]
            rows = pl.ds(0, ROWS[p])
            self.relay(p, lambda c: zrel.at[:, rows] if c is None else zrel.at[pl.ds(c * 16, 16), rows],
                       self.inbox[p].at[pl.ds((at.ring(a, -at.way) * 2 + at.core) * 16, 16), rows], T1, T1F)

    def finish(self):
        at = self.at
        for p in self.parts:
            a, rows = ORDERS[p][0], pl.ds(0, ROWS[p])
            for delta, c in self.others():
                self.arrive(p, self.inbox[p].at[pl.ds((at.ring(a, -delta) * 2 + c) * 16, 16), rows],
                            T1 + delta * 2 + c)
        self.sent()

    def read(self, c):
        return from_parts([self.inbox[p][self.table[2 * len(ORDERS) + p, c]] for p in self.parts])


class Solver:
    def __init__(self, plan, tiles_hl, x, u, r, p, p_hl, image_hl, back, z_before):
        self.plan, self.tiles_hl = plan, tiles_hl
        self.x, self.u, self.r, self.p = x, u, r, p
        self.p_hl, self.image_hl, self.back, self.z_before = p_hl, image_hl, back, z_before
        self.slots, self.blk = p_hl.shape[0], p_hl.shape[2]
        self.targets = p_hl.shape[1] // 2
        self.zero = jnp.zeros((self.targets, self.blk), F32)

    def forward(self, observed=None):
        plan, targets, blk = self.plan, self.targets, self.blk

        def tile_step(k, acc, total):
            wide = lax.dot_general(
                self.p_hl[plan[9 + 1, k]], self.tiles_hl[plan[9 + 0, k]], (((1,), (1,)), ((), ())),
                preferred_element_type=F32)
            acc = jnp.where(plan[9 + 2, k] > 0, acc, 0.0) + join(wide, targets, blk)
            if observed is not None:
                split_store(self.image_hl, k, observed[plan[9 + 4, k]] - acc)
            else:
                split_store(self.image_hl, k, acc)
                total = total + jnp.where(plan[9 + 3, k] > 0, acc * acc, 0.0)
            return acc, total

        return loop(self.slots, GROUP, tile_step, self.zero, self.zero)[1]

    def backward(self):
        plan, targets, blk = self.plan, self.targets, self.blk

        def tile_step(k, acc):
            both = self.tiles_hl[plan[9 + 5, k]]
            weights = jnp.concatenate([both[:blk], both[blk:]], axis=1)
            wide = jnp.dot(self.image_hl[plan[9 + 6, k]], weights, preferred_element_type=F32)
            acc = jnp.where(plan[9 + 7, k] > 0, acc, 0.0) + join(wide, targets, blk)
            self.back[k] = acc
            return (acc,)

        loop(self.slots, GROUP, tile_step, self.zero)

    def load_x(self):
        def one(c, _):
            split_store(self.p_hl, c, self.x[c])
            return (_,)

        loop(self.slots, 4, one, 0)

    def begin(self, first, z_of):
        def one(c, rr, gap):
            z, x, u = z_of(c), self.x[c], self.u[c]
            diff = x - z
            u_new = u + diff
            self.u[c] = u_new
            if first:
                r = self.back[self.plan[9 + 8, c]] + (z - u_new) - x
                self.z_before[c] = z
            else:
                r = self.r[c] + ((z - u_new) - (self.z_before[c] - u))
            self.r[c] = r
            self.p[c] = r
            split_store(self.p_hl, c, r)
            return rr + r * r, gap + diff * diff

        rr, gap = loop(self.slots, 4, one, self.zero, self.zero)
        self.own = rr
        self.rr = total_of(rr)
        return gap

    def length(self):
        self.a = self.rr / total_of(self.forward() + self.own)

    def move_x(self):
        p, x, a = self.p, self.x, self.a

        def move(c, _):
            x[c] = x[c] + a * p[c]
            return (_,)

        loop(self.slots, 4, move, 0)

    def move_r(self):
        p, r, back, plan, a = self.p, self.r, self.back, self.plan, self.a
        self.backward()

        def move(c, nn):
            new = r[c] - a * (back[plan[9 + 8, c]] + p[c])
            r[c] = new
            return (nn + new * new,)

        return loop(self.slots, 4, move, self.zero)[0]

    def step(self):
        p, r, x = self.p, self.r, self.x
        self.length()
        a = self.a
        nn = total_of(self.move_r())
        ratio = nn / self.rr

        def turn(c, own):
            value = p[c]
            x[c] = x[c] + a * value
            value = r[c] + ratio * value
            p[c] = value
            split_store(self.p_hl, c, value)
            return (own + value * value,)

        self.own = loop(self.slots, 4, turn, self.zero)[0]
        self.rr = nn


def fused_kernel(table, tiles_in, observed_in, x_in, u_in, x, u_out, z_own, gap_out, *scratch):
    plan = table
    (u, tiles, observed, tiles_hl, r, p, p_hl, image_hl, back, z_before, gap_box, local_sem, gap_send, gap_recv,
     send_sem, recv_sem) = scratch[BOXES * len(ORDERS):]
    boxes = [scratch[n * len(ORDERS):(n + 1) * len(ORDERS)] for n in range(BOXES)]
    loads = [pltpu.make_async_copy(src, dst, local_sem.at[n]) for n, (src, dst) in enumerate(
        ((x_in, x), (u_in, u), (tiles_in, tiles), (observed_in, observed)))]
    for load in loads:
        load.start()
    at = Place()
    barrier = pltpu.get_barrier_semaphore()
    friends = [at.partner]
    for axis in ("x", "y", "z"):
        friends += [at.near(axis, 2)] + [at.near(axis, delta, c) for delta in (1, -1) for c in (0, 1)]
    for friend in friends:
        pl.semaphore_signal(barrier, inc=1, device_id=friend, device_id_type=MESH)
    exchange = Exchange(at, table, boxes, send_sem, recv_sem)
    solver = Solver(plan, tiles_hl, x, u, r, p, p_hl, image_hl, back, z_before)
    loads[0].wait()
    loads[1].wait()
    for part in exchange.parts:
        launch = exchange.start(part, x, u)
        if part == 0:
            pl.semaphore_wait(barrier, len(friends))
        launch()
    loads[2].wait()

    def one_tile(t, _):
        split_tile(tiles_hl, t, tiles[t])
        return (_,)

    loop(tiles.shape[0], 2, one_tile, 0)
    back[back.shape[0] - 1] = solver.zero
    loads[3].wait()
    solver.load_x()
    exchange.pass_on()
    solver.forward(observed=observed)
    solver.backward()

    def rest():
        exchange.reduce_first()
        exchange.reduce_second()
        exchange.reduce_third()
        exchange.agree()
        exchange.spread_all()
        exchange.give_back()
        exchange.give_on()
        if not exchange.first:
            exchange.keep(z_own)
        exchange.finish()

    rest()
    solver.begin(True, exchange.read)

    def advance(_, carry):
        solver.rr, solver.own = carry
        solver.step()
        return solver.rr, solver.own

    solver.rr, solver.own = lax.fori_loop(0, CG_STEPS - 1, advance, (solver.rr, solver.own))
    solver.length()
    solver.move_x()
    exchange.first = False
    for part in exchange.parts:
        exchange.start(part, x, u)()
    solver.move_r()
    exchange.pass_on()
    rest()
    gap = solver.begin(False, exchange.read)
    store = pltpu.make_async_copy(u, u_out, local_sem.at[4])
    store.start()

    gap_moves = []

    def gap_copy(n, device):
        return pltpu.make_async_remote_copy(
            src_ref=gap_box.at[10 + n // 3], dst_ref=gap_box.at[n], send_sem=gap_send.at[n],
            recv_sem=gap_recv.at[n], device_id=device, device_id_type=MESH)

    def gap_stage(stage, value):
        gap_box[10 + stage] = value
        peers = [at.near("xyz"[stage], delta) for delta in (1, 2, 3)] if stage < 3 else [at.partner]
        for n, peer in enumerate(peers):
            moving = gap_copy(3 * stage + n, peer)
            moving.start()
            gap_moves.append(moving)

    def gap_sum(stage):
        value = gap_box[10 + stage]
        for n in range(3 if stage < 3 else 1):
            gap_copy(3 * stage + n, at.partner).wait_recv()
            value = value + gap_box[3 * stage + n]
        return value

    gap_stage(0, gap)
    for number in range(CG_STEPS - 1):
        solver.step()
        gap_stage(number + 1, gap_sum(number))
    solver.length()
    solver.move_x()
    gap_out[...] = gap_sum(3)
    for moving in gap_moves:
        moving.wait_send()
    store.wait()


def fused(table, tiles, observed, x, u):
    slots, targets, blk = x.shape
    count = tiles.shape[0]
    shards = table.shape[1]
    each = lambda *shape: [pltpu.VMEM(shape + (DEEP, blk), F32) for _ in ORDERS]
    scratch = (
        each(8, 16) + each(8, 16) + each(2, 16) + each(SIDE, SIDE, PER) + each(SIDE, PER) + each(2, SIDE, PER)
        + each(SIDE, PER) + each(3, PER) + each(SIDE, SIDE, PER) + each(shards) + each(shards) + each(32)
        + [pltpu.VMEM((SUB, blk), F32) for _ in ORDERS]
        + [
            pltpu.VMEM(x.shape, F32), pltpu.VMEM(tiles.shape, F32), pltpu.VMEM(observed.shape, F32),
            pltpu.VMEM((count, 2 * blk, blk), BF16), pltpu.VMEM(x.shape, F32), pltpu.VMEM(x.shape, F32),
            pltpu.VMEM((slots, 2 * targets, blk), BF16), pltpu.VMEM((count, 2 * targets, blk), BF16),
            pltpu.VMEM((count + 1, targets, blk), F32), pltpu.VMEM(x.shape, F32),
            pltpu.VMEM((14, targets, blk), F32),
            pltpu.SemaphoreType.DMA((5,)), pltpu.SemaphoreType.DMA((10,)), pltpu.SemaphoreType.DMA((10,)),
            pltpu.SemaphoreType.DMA((len(ORDERS), SEMS)), pltpu.SemaphoreType.DMA((len(ORDERS), SEMS)),
        ]
    )
    whole = pl.BlockSpec(memory_space=pltpu.VMEM)
    scalars = pl.BlockSpec(memory_space=pltpu.SMEM)
    like = jax.ShapeDtypeStruct(x.shape, F32)
    return pl.pallas_call(
        fused_kernel,
        out_shape=(like, like, jax.ShapeDtypeStruct((PER, targets, blk), F32),
                   jax.ShapeDtypeStruct((targets, blk), F32)),
        in_specs=[scalars] + [pl.BlockSpec(memory_space=pl.ANY)] * 4,
        out_specs=(whole, pl.BlockSpec(memory_space=pl.ANY), whole, whole),
        scratch_shapes=scratch,
        compiler_params=pltpu.CompilerParams(
            collective_id=0, has_side_effects=True, vmem_limit_bytes=67043328),
        name="consensus",
    )(table, tiles, observed, x, u)


def on_device(tile_data, tile_row, tile_col, tile_count, touched, owner_map, observed, start_x, start_u):
    shards = lax.axis_size(AXES)
    local_cols = touched.shape[1]
    table = tables(tile_row, tile_col, touched, owner_map, tile_count)
    flip = lambda a: jnp.swapaxes(a, 1, 2)
    x, u, z, gap = fused(table, tile_data, flip(observed), flip(start_x), flip(start_u))
    primal_gap = jnp.sqrt(jnp.sum(gap, axis=1) / (shards * local_cols * start_x.shape[1]))
    return flip(x), flip(u), flip(z), primal_gap


def solution(mesh):
    split = P(AXES)
    return jax.shard_map(
        on_device, mesh=mesh,
        in_specs=(split, split, split, split, split, P(), split, split, split),
        out_specs=(split, split, split, P()),
        check_vma=False,
    )
```

time: 187 us -> 175 us (0.936)
  Pallas kernels: 173 us -> 167 us
  other arithmetic: 5.95 us -> 1.4 us
    pallas_call x1, Pallas kernels: 173 us -> 165 us  [fused(): pl.pallas_call(fused_kernel, out_shape=(like, like, jax.ShapeDtypeStruct(...]
where the time goes in v5:
time: 175 us
  Pallas kernels  167 us (95%)
  local copies, waits for them, and re-layouts  5.29 us (3%)
    pallas_call x1, Pallas kernels, fused(): pl.pallas_call(fused_kernel, out_shape=(like, like, jax.ShapeDtypeStruct(...  165 us
    unnamed x7, local copies, waits for them, and re-layouts  5.29 us

profile of v5, /device:TPU:1, one launch (start us, length us, event | category | flops | bytes accessed | tf_op | source)
XLA Modules:
  0.0 174.9 jit_solution(2014097716810640508)
XLA Ops:
  1.3 1.6 tables.1.table
  2.9 165.4 %consensus.1 = (f32[64,64,128]{2,1,0:T(8,128)}, f32[64,64,128]{2,1,0:T(8,128)}, f32[4,64,128]{2,1,0:T(8,128)}, f32[64,128]{1,0:T(8,128)}) custom-call(s32[24,128]{1,0:T(8,128)} %tables.1.table, f32[64,128,128]{2,1,0:T(8,128)} %tiles_in.1, f32[32,64,128]{2,1,0:T(8,128)} %bitcast.11, f32[64,64,128]{2,1,0:T(8,128)} %bitcast.7, f32[64,64,128]{2,1,0:T(8,128)} %bitcast.8), custom_call_target="tpu_custom_call" | custom-call | tf_op jit(solution)/shard_map/consensus/pallas_call | solution.py:687
  168.3 0.9 reduce_sum.9
  169.1 0.5 multiply_sqrt_fusion
  169.7 0.0 copy-start
  169.7 3.3 %copy.17 = f32[64,128,64]{1,2,0:T(8,128)} copy(f32[64,128,64]{1,2,0:T(8,128)} %bitcast.10) | data formatting | bytes 4194304
  173.0 0.0 copy-done
  173.0 0.0 copy-start.1
  173.0 1.3 copy.18
  174.3 0.0 copy-done.1
  174.3 0.7 copy.19
Async XLA Ops:
  169.7 3.3 %copy-start = (f32[64,64,128]{2,1,0:T(8,128)S(1)}, f32[64,64,128]{2,1,0:T(8,128)}, u32[]{:S(2)}) copy-start(f32[64,64,128]{2,1,0:T(8,128)} %get-tuple-element.9) | copy-start | bytes 6291460
  173.0 1.3 copy-start.1

commit v6 on v5

--- a/solution.py
+++ b/solution.py
@@ -210,10 +210,12 @@
             moving.wait_send()
         self.sends = []
 
-    def pack(self, p, x, u):
+    def pack(self, p, x, u, delta):
         table, parts, mail = self.table, len(ORDERS), self.mail[p]
-
-        def record(q, _):
+        base = self.at.ring(ORDERS[p][0], delta) * 2
+
+        def record(c, _):
+            q = base + c
             for i in range(16):
                 slot = table[p, q * 16 + i]
                 for n, (one, two) in enumerate(zip(part_of(p, x, slot), part_of(p, u, slot))):
@@ -222,19 +224,23 @@
                 mail[q, i, ROWS[p]:ROWS[p] + 1, :] = jnp.full((1, x.shape[2]), tag, jnp.int32).astype(F32)
             return (_,)
 
-        loop(8, 1, record, 0)
+        loop(2, 1, record, 0)
 
     def marked(self, p):
         return pl.ds(0, ROWS[p] + (1 if self.first else 0))
 
-    def scatter(self, p, box, into, relay, base, base_f):
+    def scatter_far(self, p, box, relay, base_f):
+        at, a = self.at, ORDERS[p][0]
+        self.go(p, box(at.ring(a, 2), None), relay, base_f, base_f, at.near(a, at.way))
+
+    def scatter_near(self, p, delta, box, into, base):
         at, a, core = self.at, ORDERS[p][0], self.at.core
-        self.go(p, box(at.ring(a, 2), None), relay, base_f, base_f, at.near(a, at.way))
-        for delta in (1, 3):
+        if delta:
             for c in (0, 1):
                 self.go(p, box(at.ring(a, delta), c), into(delta), base + delta * 2 + c,
                         base + delta * 2 + core, at.near(a, delta, c))
-        self.go(p, box(at.me[a], 1 - core), into(0), base, base + core, at.partner)
+        else:
+            self.go(p, box(at.me[a], 1 - core), into(0), base, base + core, at.partner)
 
     def relay(self, p, relay, into, base, base_f):
         at, a = self.at, ORDERS[p][0]
@@ -242,17 +248,21 @@
         for c in (0, 1):
             self.go(p, relay(c), into, base + 4 + c, base + 4 + at.core, at.near(a, at.way, c))
 
-    def start(self, p, x, u):
-        self.pack(p, x, u)
-
-        rows = self.marked(p)
-
-        def box(place, c):
-            return self.mail[p].at[pl.ds(place * 2, 2) if c is None else place * 2 + c, :, rows]
-
-        return lambda: self.scatter(
-            p, box, lambda delta: self.in1[p].at[delta * 2 + self.at.core, :, rows], self.fwd1[p].at[:, :, rows],
-            S1, S1F)
+    def start(self, x, u, ready=lambda: None):
+        def box(p, place, c):
+            return self.mail[p].at[pl.ds(place * 2, 2) if c is None else place * 2 + c, :, self.marked(p)]
+
+        for p in self.parts:
+            self.pack(p, x, u, 2)
+            if p == 0:
+                ready()
+            self.scatter_far(p, functools.partial(box, p), self.fwd1[p].at[:, :, self.marked(p)], S1F)
+        for delta in (1, 3, 0):
+            for p in self.parts:
+                self.pack(p, x, u, delta)
+                self.scatter_near(
+                    p, delta, functools.partial(box, p),
+                    lambda delta: self.in1[p].at[delta * 2 + self.at.core, :, self.marked(p)], S1)
 
     def pass_on(self):
         for p in self.parts:
@@ -424,7 +434,9 @@
                 return sel.at[pl.ds(place * 32, 32) if c is None else pl.ds((place * 2 + c) * 16, 16), rows]
 
             mine = self.inbox[p].at[pl.ds((at.me[a] * 2 + at.core) * 16, 16), rows]
-            self.scatter(p, box, lambda delta: mine, self.zrel[p].at[:, rows], T1, T1F)
+            self.scatter_far(p, box, self.zrel[p].at[:, rows], T1F)
+            for delta in (1, 3, 0):
+                self.scatter_near(p, delta, box, lambda delta: mine, T1)
 
     def give_on(self):
         at = self.at
@@ -576,11 +588,7 @@
     solver = Solver(plan, tiles_hl, x, u, r, p, p_hl, image_hl, back, z_before)
     loads[0].wait()
     loads[1].wait()
-    for part in exchange.parts:
-        launch = exchange.start(part, x, u)
-        if part == 0:
-            pl.semaphore_wait(barrier, len(friends))
-        launch()
+    exchange.start(x, u, lambda: pl.semaphore_wait(barrier, len(friends)))
     loads[2].wait()
 
     def one_tile(t, _):
@@ -619,8 +627,7 @@
     solver.length()
     solver.move_x()
     exchange.first = False
-    for part in exchange.parts:
-        exchange.start(part, x, u)()
+    exchange.start(x, u)
     solver.move_r()
     exchange.pass_on()
     rest()
@@ -628,38 +635,74 @@
     store = pltpu.make_async_copy(u, u_out, local_sem.at[4])
     store.start()
 
-    gap_moves = []
-
-    def gap_copy(n, device):
+    def gap_copy(n, stage, device):
         return pltpu.make_async_remote_copy(
-            src_ref=gap_box.at[10 + n // 3], dst_ref=gap_box.at[n], send_sem=gap_send.at[n],
+            src_ref=gap_box.at[10 + stage], dst_ref=gap_box.at[n], send_sem=gap_send.at[n],
             recv_sem=gap_recv.at[n], device_id=device, device_id_type=MESH)
 
-    def gap_stage(stage, value):
-        gap_box[10 + stage] = value
-        peers = [at.near("xyz"[stage], delta) for delta in (1, 2, 3)] if stage < 3 else [at.partner]
-        for n, peer in enumerate(peers):
-            moving = gap_copy(3 * stage + n, peer)
+    def gap_peer(stage, delta):
+        along = {"x": (1 - stage) * (2 - stage) // 2, "y": stage * (2 - stage), "z": stage * (stage - 1) // 2}
+        to = {a: lax.rem(at.me[a] + delta * along[a], SIDE) for a in along}
+        return ((to["y"] * SIDE + to["x"]) * 2 + at.core, to["z"])
+
+    def gap_step(stage, carry):
+        solver.rr, solver.own = carry
+        moves = [gap_copy(3 * stage + delta - 1, stage, gap_peer(stage, delta)) for delta in (1, 2, 3)]
+        for moving in moves:
             moving.start()
-            gap_moves.append(moving)
-
-    def gap_sum(stage):
+        solver.step()
         value = gap_box[10 + stage]
-        for n in range(3 if stage < 3 else 1):
-            gap_copy(3 * stage + n, at.partner).wait_recv()
+        for n, moving in enumerate(moves):
+            moving.wait()
             value = value + gap_box[3 * stage + n]
-        return value
-
-    gap_stage(0, gap)
-    for number in range(CG_STEPS - 1):
-        solver.step()
-        gap_stage(number + 1, gap_sum(number))
+        gap_box[11 + stage] = value
+        return solver.rr, solver.own
+
+    gap_box[10] = gap
+    solver.rr, solver.own = lax.fori_loop(0, CG_STEPS - 1, gap_step, (solver.rr, solver.own))
+    moving = gap_copy(9, 3, at.partner)
+    moving.start()
     solver.length()
     solver.move_x()
-    gap_out[...] = gap_sum(3)
-    for moving in gap_moves:
-        moving.wait_send()
+    moving.wait()
+    gap_out[...] = gap_box[13] + gap_box[9]
     store.wait()
+
+
+def hand_over_kernel(scale, x_in, u_in, z_in, gap, x, u, z, primal, x_box, u_box, z_box, sems):
+    step = x_in.shape[0] // 4
+    moves = [(z_in, z_box, z)]
+    for n in range(4):
+        rows = pl.ds(n * step, step)
+        moves += [(a.at[rows], b.at[rows], c.at[rows]) for a, b, c in ((x_in, x_box, x), (u_in, u_box, u))]
+    reads = [pltpu.make_async_copy(a, b, sems.at[0, n]) for n, (a, b, _) in enumerate(moves)]
+    writes = [pltpu.make_async_copy(b, c, sems.at[1, n]) for n, (_, b, c) in enumerate(moves)]
+    for read in reads:
+        read.start()
+    targets, blk = gap.shape
+    down, across = (lax.broadcasted_iota(jnp.int32, (targets, blk), n) for n in (0, 1))
+    total = jnp.sum(gap[...], axis=1, keepdims=True)
+    total = jnp.sum(jnp.where(down == across, total, 0.0), axis=0, keepdims=True)
+    primal[...] = jnp.sqrt(total / scale)
+    for read, write in zip(reads, writes):
+        read.wait()
+        write.start()
+    for write in writes:
+        write.wait()
+
+
+def hand_over(scale, x, u, z, gap):
+    anywhere, whole = pl.BlockSpec(memory_space=pl.ANY), pl.BlockSpec(memory_space=pltpu.VMEM)
+    like = [jax.ShapeDtypeStruct(a.shape, F32) for a in (x, u, z)]
+    return pl.pallas_call(
+        functools.partial(hand_over_kernel, float(scale)),
+        out_shape=(*like, jax.ShapeDtypeStruct((1, gap.shape[1]), F32)),
+        in_specs=[anywhere] * 3 + [whole],
+        out_specs=(anywhere, anywhere, anywhere, whole),
+        scratch_shapes=[pltpu.VMEM(a.shape, F32) for a in (x, u, z)] + [pltpu.SemaphoreType.DMA((2, 9))],
+        compiler_params=pltpu.CompilerParams(vmem_limit_bytes=67043328),
+        name="hand_over",
+    )(x, u, z, gap)
 
 
 def fused(table, tiles, observed, x, u):
@@ -703,8 +746,8 @@
     table = tables(tile_row, tile_col, touched, owner_map, tile_count)
     flip = lambda a: jnp.swapaxes(a, 1, 2)
     x, u, z, gap = fused(table, tile_data, flip(observed), flip(start_x), flip(start_u))
-    primal_gap = jnp.sqrt(jnp.sum(gap, axis=1) / (shards * local_cols * start_x.shape[1]))
-    return flip(x), flip(u), flip(z), primal_gap
+    x, u, z, primal = hand_over(shards * local_cols * start_x.shape[1], x, u, z, gap)
+    return flip(x), flip(u), flip(z), primal[0, :start_x.shape[2]]
 
 
 def solution(mesh):

time: 175 us -> 175 us (level)
  Pallas kernels: 167 us -> 173 us
  local copies, waits for them, and re-layouts: 5.29 us -> 1.12 us
    unnamed x7 -> x0, local copies, waits for them, and re-layouts: 5.29 us -> none
    pallas_call x0 -> x1, Pallas kernels: none -> 5.09 us  [hand_over(): pl.pallas_call(functools.partial(hand_over_kernel, float(scale)), out_sha...]
where the time goes in v6:
time: 175 us
  Pallas kernels  173 us (99%)
    pallas_call x1, Pallas kernels, fused(): pl.pallas_call(fused_kernel, out_shape=(like, like, jax.ShapeDtypeStruct(...  166 us
    pallas_call x1, Pallas kernels, hand_over(): pl.pallas_call(functools.partial(hand_over_kernel, float(scale)), out_sha...  5.09 us

profile of v6, /device:TPU:1, one launch (start us, length us, event | category | flops | bytes accessed | tf_op | source)
XLA Modules:
  0.0 175.0 jit_solution(15437456199352391256)
XLA Ops:
  1.3 1.6 tables.1.table
  2.9 165.9 %consensus.1 = (f32[64,64,128]{2,1,0:T(8,128)}, f32[64,64,128]{2,1,0:T(8,128)}, f32[4,64,128]{2,1,0:T(8,128)}, f32[64,128]{1,0:T(8,128)}) custom-call(s32[24,128]{1,0:T(8,128)} %tables.1.table, f32[64,128,128]{2,1,0:T(8,128)} %tiles_in.1, f32[32,64,128]{2,1,0:T(8,128)} %bitcast.11, f32[64,64,128]{2,1,0:T(8,128)} %bitcast.9, f32[64,64,128]{2,1,0:T(8,128)} %bitcast.10), custom_call_target="tpu_custom_call" | custom-call | tf_op jit(solution)/shard_map/consensus/pallas_call | solution.py:730
  168.8 5.1 %hand_over.1 = (f32[64,64,128]{2,1,0:T(8,128)}, f32[64,64,128]{2,1,0:T(8,128)}, f32[4,64,128]{2,1,0:T(8,128)}, f32[1,128]{1,0:T(1,128)}) custom-call(f32[64,64,128]{2,1,0:T(8,128)} %get-tuple-element.12.x_in, f32[64,64,128]{2,1,0:T(8,128)} %get-tuple-element.13.u_in, f32[4,64,128]{2,1,0:T(8,128)} %get-tuple-element.14.z_in, f32[64,128]{1,0:T(8,128)} %get-tuple-element.15.gap), custom_call_target="tpu_custom_call" | custom-call | tf_op jit(solution)/shard_map/hand_over/pallas_call | solution.py:697
  173.9 1.1 slice_bitcast_fusion

commit v7 on v6

--- a/solution.py
+++ b/solution.py
@@ -281,13 +281,15 @@
     def others(self):
         return ((1, 0), (1, 1), (3, 0), (3, 1), (0, 1 - self.at.core), (2, 0), (2, 1))
 
-    def combine(self, p):
+    def combine(self, p, far):
+        at, b = self.at, ORDERS[p][1]
         found = self.sources(p)
         part2 = self.part2[p]
         blk = part2.shape[4]
         mark = ROWS[p] - 2 * SUB
 
-        def some(a2, _):
+        def some(n, _):
+            a2 = at.ring(b, 2) if far else at.ring(b, at.way * (n - 1))
             for a3 in range(SIDE):
                 i = a2 * SIDE + a3
                 tags = [jnp.broadcast_to(read(i, pl.ds(ROWS[p], 1)), (SUB, blk)) for _, _, read in found]
@@ -302,7 +304,10 @@
                         part2[a2, a3, k, j * SUB:(j + 1) * SUB, :] = value
             return (_,)
 
-        loop(SIDE, 1, some, 0)
+        if far:
+            some(0, 0)
+        else:
+            loop(SIDE - 1, 1, some, 0)
 
     def reduce_first(self):
         at = self.at
@@ -311,11 +316,15 @@
             rows = self.marked(p)
             for delta, c in self.others():
                 self.arrive(p, self.in1[p].at[delta * 2 + c, :, rows], S1 + delta * 2 + c)
-            self.combine(p)
+            self.combine(p, True)
             for n, delta in enumerate(THERE):
                 piece = at.ring(d, delta)
                 self.go(p, self.part2[p].at[at.ring(b, 2), piece, :, rows], self.fwd2[p].at[piece, :, rows],
                         S2F + n, S2F + n, at.near(b, at.way))
+        for p in self.parts:
+            b, d = ORDERS[p][1], ORDERS[p][2]
+            rows = self.marked(p)
+            self.combine(p, False)
             for n, delta in enumerate(THERE):
                 piece = at.ring(d, delta)
                 self.go(p, self.part2[p].at[at.ring(b, -at.way), piece, :, rows], self.in2[p].at[1, piece, :, rows],
@@ -393,7 +402,7 @@
             for p in self.parts:
                 act(p, n)
 
-    def select(self, p):
+    def select(self, p, far):
         at = self.at
         a = ORDERS[p][0]
         found = self.sources(p)
@@ -405,6 +414,8 @@
                 i = a2 * SIDE + a3
                 blocks = [[zb2[a2, a3, k, rows, :] for rows in tiles] for k in range(PER)]
                 for number, (delta, c, read) in enumerate(found):
+                    if (delta == 2) != far:
+                        continue
                     tag = jnp.broadcast_to(read(i, pl.ds(ROWS[p], 1)), blocks[0][0].shape)
                     hit = [tag == float(k) for k in range(PER - 1)]
                     for j, rows in enumerate(tiles):
@@ -427,16 +438,18 @@
                 piece = at.ring(ORDERS[p][2], -delta)
                 self.arrive(p, self.zb2[p].at[at.ring(b, at.way), piece, :, rows], T2D + n)
                 self.arrive(p, self.zb2[p].at[at.ring(b, 2), piece, :, rows], T2F + n)
-            self.select(p)
-            sel = self.sel[p]
-
-            def box(place, c):
-                return sel.at[pl.ds(place * 32, 32) if c is None else pl.ds((place * 2 + c) * 16, 16), rows]
-
+            self.select(p, True)
+            self.scatter_far(p, functools.partial(self.sel_box, p), self.zrel[p].at[:, rows], T1F)
+        for p in self.parts:
+            a, rows = ORDERS[p][0], pl.ds(0, ROWS[p])
             mine = self.inbox[p].at[pl.ds((at.me[a] * 2 + at.core) * 16, 16), rows]
-            self.scatter_far(p, box, self.zrel[p].at[:, rows], T1F)
+            self.select(p, False)
             for delta in (1, 3, 0):
-                self.scatter_near(p, delta, box, lambda delta: mine, T1)
+                self.scatter_near(p, delta, functools.partial(self.sel_box, p), lambda delta: mine, T1)
+
+    def sel_box(self, p, place, c):
+        records = pl.ds(place * 32, 32) if c is None else pl.ds((place * 2 + c) * 16, 16)
+        return self.sel[p].at[records, pl.ds(0, ROWS[p])]
 
     def give_on(self):
         at = self.at
@@ -503,7 +516,7 @@
             split_store(self.p_hl, c, self.x[c])
             return (_,)
 
-        loop(self.slots, 4, one, 0)
+        loop(self.slots, 8, one, 0)
 
     def begin(self, first, z_of):
         def one(c, rr, gap):
@@ -521,7 +534,7 @@
             split_store(self.p_hl, c, r)
             return rr + r * r, gap + diff * diff
 
-        rr, gap = loop(self.slots, 4, one, self.zero, self.zero)
+        rr, gap = loop(self.slots, 8, one, self.zero, self.zero)
         self.own = rr
         self.rr = total_of(rr)
         return gap
@@ -536,7 +549,7 @@
             x[c] = x[c] + a * p[c]
             return (_,)
 
-        loop(self.slots, 4, move, 0)
+        loop(self.slots, 8, move, 0)
 
     def move_r(self):
         p, r, back, plan, a = self.p, self.r, self.back, self.plan, self.a
@@ -547,7 +560,7 @@
             r[c] = new
             return (nn + new * new,)
 
-        return loop(self.slots, 4, move, self.zero)[0]
+        return loop(self.slots, 8, move, self.zero)[0]
 
     def step(self):
         p, r, x = self.p, self.r, self.x
@@ -564,7 +577,7 @@
             split_store(self.p_hl, c, value)
             return (own + value * value,)
 
-        self.own = loop(self.slots, 4, turn, self.zero)[0]
+        self.own = loop(self.slots, 8, turn, self.zero)[0]
         self.rr = nn
 
 
@@ -683,7 +696,7 @@
     down, across = (lax.broadcasted_iota(jnp.int32, (targets, blk), n) for n in (0, 1))
     total = jnp.sum(gap[...], axis=1, keepdims=True)
     total = jnp.sum(jnp.where(down == across, total, 0.0), axis=0, keepdims=True)
-    primal[...] = jnp.sqrt(total / scale)
+    primal[...] = jnp.sqrt(total / scale)[:, :targets]
     for read, write in zip(reads, writes):
         read.wait()
         write.start()
@@ -696,7 +709,7 @@
     like = [jax.ShapeDtypeStruct(a.shape, F32) for a in (x, u, z)]
     return pl.pallas_call(
         functools.partial(hand_over_kernel, float(scale)),
-        out_shape=(*like, jax.ShapeDtypeStruct((1, gap.shape[1]), F32)),
+        out_shape=(*like, jax.ShapeDtypeStruct((1, gap.shape[0]), F32)),
         in_specs=[anywhere] * 3 + [whole],
         out_specs=(anywhere, anywhere, anywhere, whole),
         scratch_shapes=[pltpu.VMEM(a.shape, F32) for a in (x, u, z)] + [pltpu.SemaphoreType.DMA((2, 9))],
@@ -747,7 +760,7 @@
     flip = lambda a: jnp.swapaxes(a, 1, 2)
     x, u, z, gap = fused(table, tile_data, flip(observed), flip(start_x), flip(start_u))
     x, u, z, primal = hand_over(shards * local_cols * start_x.shape[1], x, u, z, gap)
-    return flip(x), flip(u), flip(z), primal[0, :start_x.shape[2]]
+    return flip(x), flip(u), flip(z), primal[0]
 
 
 def solution(mesh):

time: 175 us -> 173 us (0.989)
  no operation moved by 1% of the time
where the time goes in v7:
time: 173 us
  Pallas kernels  172 us (99%)
    pallas_call x1, Pallas kernels, fused(): pl.pallas_call(fused_kernel, out_shape=(like, like, jax.ShapeDtypeStruct(...  165 us
    pallas_call x1, Pallas kernels, hand_over(): pl.pallas_call(functools.partial(hand_over_kernel, float(scale)), out_sha...  5.08 us

profile of v7, /device:TPU:1, one launch (start us, length us, event | category | flops | bytes accessed | tf_op | source)
XLA Modules:
  0.0 173.1 jit_solution(380193681122960303)
XLA Ops:
  1.3 1.6 tables.1.table
  2.9 164.9 %consensus.1 = (f32[64,64,128]{2,1,0:T(8,128)}, f32[64,64,128]{2,1,0:T(8,128)}, f32[4,64,128]{2,1,0:T(8,128)}, f32[64,128]{1,0:T(8,128)}) custom-call(s32[24,128]{1,0:T(8,128)} %tables.1.table, f32[64,128,128]{2,1,0:T(8,128)} %tiles_in.1, f32[32,64,128]{2,1,0:T(8,128)} %bitcast.10, f32[64,64,128]{2,1,0:T(8,128)} %bitcast.8, f32[64,64,128]{2,1,0:T(8,128)} %bitcast.9), custom_call_target="tpu_custom_call" | custom-call | tf_op jit(solution)/shard_map/consensus/pallas_call | solution.py:743
  167.8 5.1 %hand_over.1 = (f32[64,64,128]{2,1,0:T(8,128)}, f32[64,64,128]{2,1,0:T(8,128)}, f32[4,64,128]{2,1,0:T(8,128)}, f32[1,64]{1,0:T(1,128)}) custom-call(f32[64,64,128]{2,1,0:T(8,128)} %get-tuple-element.12.x_in, f32[64,64,128]{2,1,0:T(8,128)} %get-tuple-element.13.u_in, f32[4,64,128]{2,1,0:T(8,128)} %get-tuple-element.14.z_in, f32[64,128]{1,0:T(8,128)} %get-tuple-element.15.gap), custom_call_target="tpu_custom_call" | custom-call | tf_op jit(solution)/shard_map/hand_over/pallas_call | solution.py:710

commit v8 on v7

--- a/solution.py
+++ b/solution.py
@@ -516,7 +516,7 @@
             split_store(self.p_hl, c, self.x[c])
             return (_,)
 
-        loop(self.slots, 8, one, 0)
+        loop(self.slots, 16, one, 0)
 
     def begin(self, first, z_of):
         def one(c, rr, gap):
@@ -534,7 +534,7 @@
             split_store(self.p_hl, c, r)
             return rr + r * r, gap + diff * diff
 
-        rr, gap = loop(self.slots, 8, one, self.zero, self.zero)
+        rr, gap = loop(self.slots, 16, one, self.zero, self.zero)
         self.own = rr
         self.rr = total_of(rr)
         return gap
@@ -549,7 +549,7 @@
             x[c] = x[c] + a * p[c]
             return (_,)
 
-        loop(self.slots, 8, move, 0)
+        loop(self.slots, 16, move, 0)
 
     def move_r(self):
         p, r, back, plan, a = self.p, self.r, self.back, self.plan, self.a
@@ -560,7 +560,7 @@
             r[c] = new
             return (nn + new * new,)
 
-        return loop(self.slots, 8, move, self.zero)[0]
+        return loop(self.slots, 16, move, self.zero)[0]
 
     def step(self):
         p, r, x = self.p, self.r, self.x
@@ -577,7 +577,7 @@
             split_store(self.p_hl, c, value)
             return (own + value * value,)
 
-        self.own = loop(self.slots, 8, turn, self.zero)[0]
+        self.own = loop(self.slots, 16, turn, self.zero)[0]
         self.rr = nn
 
 

time: 173 us -> 173 us (level)
  no operation moved by 1% of the time
where the time goes in v8:
time: 173 us
  Pallas kernels  171 us (99%)
    pallas_call x1, Pallas kernels, fused(): pl.pallas_call(fused_kernel, out_shape=(like, like, jax.ShapeDtypeStruct(...  165 us
    pallas_call x1, Pallas kernels, hand_over(): pl.pallas_call(functools.partial(hand_over_kernel, float(scale)), out_sha...  5.08 us

profile of v8, /device:TPU:1, one launch (start us, length us, event | category | flops | bytes accessed | tf_op | source)
XLA Modules:
  0.0 172.7 jit_solution(10294483308427430269)
XLA Ops:
  1.3 1.6 tables.1.table
  2.9 164.6 %consensus.1 = (f32[64,64,128]{2,1,0:T(8,128)}, f32[64,64,128]{2,1,0:T(8,128)}, f32[4,64,128]{2,1,0:T(8,128)}, f32[64,128]{1,0:T(8,128)}) custom-call(s32[24,128]{1,0:T(8,128)} %tables.1.table, f32[64,128,128]{2,1,0:T(8,128)} %tiles_in.1, f32[32,64,128]{2,1,0:T(8,128)} %bitcast.10, f32[64,64,128]{2,1,0:T(8,128)} %bitcast.8, f32[64,64,128]{2,1,0:T(8,128)} %bitcast.9), custom_call_target="tpu_custom_call" | custom-call | tf_op jit(solution)/shard_map/consensus/pallas_call | solution.py:743
  167.5 5.1 %hand_over.1 = (f32[64,64,128]{2,1,0:T(8,128)}, f32[64,64,128]{2,1,0:T(8,128)}, f32[4,64,128]{2,1,0:T(8,128)}, f32[1,64]{1,0:T(1,128)}) custom-call(f32[64,64,128]{2,1,0:T(8,128)} %get-tuple-element.12.x_in, f32[64,64,128]{2,1,0:T(8,128)} %get-tuple-element.13.u_in, f32[4,64,128]{2,1,0:T(8,128)} %get-tuple-element.14.z_in, f32[64,128]{1,0:T(8,128)} %get-tuple-element.15.gap), custom_call_target="tpu_custom_call" | custom-call | tf_op jit(solution)/shard_map/hand_over/pallas_call | solution.py:710
